TPU v7x, 128 devices: a whole 4x4x4 slice. The times are simulated.
128 devices in a mesh: seq: 64 (over y, z, x), fsdp: 2 (over core).
Axes of the slice: x: 4, y: 4, z: 4, core: 2. Of those that a mesh axis runs over, the one named last changes fastest.
Arguments:
- tokens: bfloat16 [2, 49152, 2560], P('fsdp', 'seq'), may hold values from -6 to 6
- bounds: int32 [2, 64, 2], P('fsdp', 'seq'), may hold values from 0 to 96, as said below
- in_weight: bfloat16 [2560, 5416], P(('seq', 'fsdp')), may hold values from -0.125 to 0.125
- conv_weight: float32 [4, 2816], replicated, may hold values from -0.6 to 0.6
- conv_bias: float32 [2816], replicated, may hold values from -3 to 3
- dt_bias: float32 [40], replicated, may hold values from -4 to 0
- decay_rate: float32 [40], replicated, may hold values from 1.2207031e-05 to 0.5
- skip_gain: float32 [40], replicated, may hold values from 0.1 to 1.9
- norm_gain: float32 [2560], replicated, may hold values from 0.1 to 1.9
Outputs:
- layer_out: bfloat16 [2, 49152, 2560], P('fsdp', 'seq')
Inputs may be any that keep to these rules, and one draw needn't show every extreme that they name: For sequence b, bounds[b, s] holds the first and one past the last block of the shard of index s of seq; shards are consecutive in s and cover all 96 blocks; each holds 1 to 3 blocks, and some shard holds 3.
All inputs are finite; a program needn't handle non-finite values.
Results may differ from a plain program's by a relative error of at most 0.0028.
The roundings to bfloat16 on the way count: a program that leaves them out, or rounds other values in their place, can miss the bound.
Values may be sent and summed in bfloat16 or wider, within the bound.
A program may use at most 192 MiB of HBM per device.

v0:
```python
import jax
import jax.numpy as jnp
from jax import lax
from jax.sharding import Mesh
from jax.sharding import PartitionSpec as P

BLOCK = 256
SEQ_FSDP = ("seq_0", "seq_1", "seq_2", "fsdp")
SEQ = ("seq_0", "seq_1", "seq_2")


def passed_along(value, axis, steps):
    count = lax.axis_size(axis)
    leading, last = (max(0, -steps), min(count, count - steps))
    return lax.ppermute(value, axis, [(source, source + steps) for source in range(leading, last)])


def filled_with(shard, identity):
    return jax.tree.map(
        lambda part, zero: jnp.zeros_like(part) + jnp.asarray(zero, part.dtype), shard, identity
    )


def prefix_by_axis(shard, axes, combine, identity):
    before = start = filled_with(shard, identity)
    total = shard
    for axis in reversed(axes):
        length, place = (lax.axis_size(axis), lax.axis_index(axis))
        pieces = jax.tree.map(lambda part: lax.all_gather(part, axis), total)
        inside, total = (start, start)
        for k in range(length):
            passed = k < place
            total = combine(total, jax.tree.map(lambda part: part[k], pieces))
            inside = jax.tree.map(lambda new, old: jnp.where(passed, new, old), total, inside)
        before = combine(inside, before)
    return before


def block_terms(head_input, input_map, output_map, step_size, decay_rate):
    log_decay = -(step_size * decay_rate[None, :]).T
    cumulative = jnp.cumsum(log_decay, axis=1)
    pairwise = cumulative[:, :, None] - cumulative[:, None, :]
    length = cumulative.shape[1]
    causal = jnp.arange(length)[:, None] >= jnp.arange(length)[None, :]
    pair_decay = jnp.exp(jnp.where(causal[None], pairwise, -jnp.inf))
    scores = jnp.dot(output_map, input_map.T, preferred_element_type=jnp.float32)
    mixing = scores[None] * pair_decay * step_size.T[:, None, :]
    inner_out = jnp.einsum("hij,jhp->ihp", mixing, head_input, precision=lax.Precision.HIGH)
    to_end = jnp.exp(cumulative[:, -1:] - cumulative) * step_size.T
    local_state = jnp.einsum(
        "hj,jhp,jn->hpn",
        to_end,
        head_input,
        input_map.astype(jnp.float32),
        precision=lax.Precision.HIGH,
    )
    return (inner_out, cumulative, local_state)


def carried(output_map, cumulative, state):
    reach = jnp.einsum(
        "in,hpn->ihp", output_map.astype(jnp.float32), state, precision=lax.Precision.HIGH
    )
    return jnp.exp(cumulative).T[:, :, None] * reach


def compose(earlier, later):
    return (earlier[0] * later[0], later[0][:, None, None] * earlier[1] + later[1])


def local(
    tokens, bounds, in_weight, conv_weight, conv_bias, dt_bias, decay_rate, skip_gain, norm_gain
):
    slots = tokens.shape[1]
    inner = norm_gain.shape[0]
    state_width = (conv_bias.shape[0] - inner) // 2
    heads = decay_rate.shape[0]
    head_dim = inner // heads
    kernel = conv_weight.shape[0]
    capacity = slots // BLOCK
    shard_blocks = bounds[0, 0, 1] - bounds[0, 0, 0]
    own_rows = tokens[0]
    summed = jnp.dot(
        own_rows,
        lax.all_gather(in_weight, SEQ_FSDP, axis=0, tiled=True),
        preferred_element_type=jnp.float32,
    )
    projected = summed.astype(jnp.bfloat16)
    gate = projected[:, :inner].astype(jnp.float32)
    mixed_in = projected[:, inner : 2 * inner + 2 * state_width]
    raw_step = projected[:, 2 * inner + 2 * state_width :].astype(jnp.float32)
    edge_rows = lax.dynamic_slice_in_dim(
        mixed_in, shard_blocks * BLOCK - (kernel - 1), kernel - 1, 0
    )
    previous = passed_along(edge_rows, SEQ, 1)
    extended = jnp.concatenate([previous, mixed_in], axis=0)
    convolved = jnp.zeros((slots, mixed_in.shape[1]), jnp.float32) + conv_bias[None, :]
    for offset in range(kernel):
        convolved = convolved + conv_weight[offset][None, :] * extended[
            offset : offset + slots
        ].astype(jnp.float32)
    conv_out = jax.nn.silu(convolved).astype(jnp.bfloat16)
    live_mask = jnp.arange(slots)[:, None] < shard_blocks * BLOCK
    step_size = jnp.where(live_mask, jax.nn.softplus(raw_step + dt_bias[None, :]), 0.0)
    pieces = []
    decay_total = jnp.ones((heads,), jnp.float32)
    summary_state = jnp.zeros((heads, head_dim, state_width), jnp.float32)
    for place in range(capacity):
        lower = place * BLOCK
        upper = lower + BLOCK
        in_values = (
            conv_out[lower:upper, :inner].astype(jnp.float32).reshape(BLOCK, heads, head_dim)
        )
        in_map = conv_out[lower:upper, inner : inner + state_width]
        out_map = conv_out[lower:upper, inner + state_width :]
        inner_out, cumulative, local_state = block_terms(
            in_values, in_map, out_map, step_size[lower:upper], decay_rate
        )
        block_decay = jnp.exp(cumulative[:, -1])
        summary_state = block_decay[:, None, None] * summary_state + local_state
        decay_total = decay_total * block_decay
        pieces.append((in_values, out_map, inner_out, cumulative, local_state, block_decay))
    identity = (
        jnp.ones((heads,), jnp.float32),
        jnp.zeros((heads, head_dim, state_width), jnp.float32),
    )
    incoming = prefix_by_axis((decay_total, summary_state), SEQ, compose, identity)
    state = incoming[1]
    results = []
    for in_values, out_map, inner_out, cumulative, local_state, block_decay in pieces:
        result = (
            inner_out + carried(out_map, cumulative, state) + skip_gain[None, :, None] * in_values
        )
        results.append(result.reshape(BLOCK, inner))
        state = block_decay[:, None, None] * state + local_state
    scanned = jnp.concatenate(results, axis=0)
    gated = scanned * jax.nn.silu(gate)
    normed = (
        gated
        * lax.rsqrt(jnp.mean(gated * gated, axis=1, keepdims=True) + 1e-05)
        * norm_gain[None, :]
    )
    layer_out = jnp.where(live_mask, normed, 0.0).astype(jnp.bfloat16)
    return layer_out[None]


def solution(mesh):
    split = Mesh(
        mesh.devices.reshape(4, 4, 4, mesh.shape["fsdp"]), ("seq_0", "seq_1", "seq_2", "fsdp")
    )
    return jax.shard_map(
        local,
        mesh=split,
        in_specs=(
            P("fsdp", SEQ, None),
            P("fsdp", SEQ, None),
            P(SEQ_FSDP, None),
            P(),
            P(),
            P(),
            P(),
            P(),
            P(),
        ),
        out_specs=P("fsdp", SEQ, None),
        check_vma=False,
    )
```

profile of v0, /device:TPU:1, one launch (start us, length us, event | category | flops | bytes accessed | tf_op | source)
XLA Modules:
  0.0 452.2 jit_solution(928340942018903259)
XLA Ops:
  7.3 1.4 fusion.109
  10.0 1.1 slice_reduce_fusion.9
  11.1 109.3 %all-gather.16.cloned.1.call-done = bf16[128,20,5416]{2,1,0:T(8,128)(2,1)} async-done(((bf16[1,20,5416]{2,1,0:T(8,128)(2,1)}), bf16[128,20,5416]{2,1,0:T(8,128)(2,1)}) %all-gather.16.cloned.1.call-update) | async-done | bytes 27729936 | tf_op jit(solution)/shard_map/all_gather | solution.py:85
  120.4 36.9 %reshape.339 = bf16[2560,5416]{1,0:T(8,128)(2,1)} reshape(bf16[128,20,5416]{2,1,0:T(8,128)(2,1)} %all-gather.16.cloned.1.call-done) | data formatting | bytes 55459840
  157.3 29.0 %convolution_convert_fusion = bf16[768,5416]{0,1:T(8,128)(2,1)} fusion(bf16[2560,5416]{1,0:T(8,128)(2,1)} %reshape.339, bf16[1,768,2560]{2,1,0:T(8,128)(2,1)} %param.9), kind=kOutput, calls=%fused_computation.18 | convolution fusion | flops 21300738048 | bytes 39981056 | tf_op jit(solution)/shard_map/dot_general | solution.py:83
  186.2 2.5 slice.251
  188.8 2.0 copy-done
  191.3 3.3 collective-permute-start
  194.6 1.0 fusion.78
  200.9 16.0 %multiply_convert_fusion = bf16[768,2816]{0,1:T(8,128)(2,1)S(1)} fusion(bf16[768,2816]{0,1:T(8,128)(2,1)} %copy-done, bf16[3,2816]{0,1:T(8,128)(2,1)S(1)} %copy.37, f32[2816]{0:T(1024)S(1)} %get-tuple-element.7, f32[2816]{0:T(1024)S(1)} %get-tuple-element.8, f32[2816]{0:T(1024)S(1)} %get-tuple-element.6, f32[2816]{0:T(1024)S(1)} %get-tuple-element.5, ...), kind=kLoop, calls=%fused_computation.21 | loop fusion | flops 56229888 | bytes 8723968 | tf_op jit(solution)/shard_map/convert_element_type | solution.py:102
  220.3 1.9 fusion.56
  223.7 7.7 %all-reduce = f32[160]{0:T(256)S(1)} all-reduce(f32[160]{0:T(256)S(1)} %dynamic-update-slice), channel_id=2, replica_groups=mesh['seq_0'=4,'seq_1'=4,'seq_2'=4,'fsdp'=2] {'seq_2'}, use_global_device_ids=true, to_apply=%add | all-reduce | flops 160 | bytes 1280
  231.5 8.7 %all-gather.3 = f32[4,1,40]{2,1,0:T(1,128)S(1)} all-gather(f32[1,1,40]{2,1,0:T(1,128)S(1)} %get-tuple-element.46), channel_id=1, replica_groups=mesh['seq_0'=4,'seq_1'=4,'seq_2'=4,'fsdp'=2] {'seq_1'}, dimensions={0}, use_global_device_ids=true | all-gather | bytes 800 | tf_op jit(solution)/shard_map/all_gather | solution.py:29
  240.8 38.4 %all-gather.14.cloned.1.call-done = f32[160,64,128]{2,1,0:T(8,128)} async-done(((f32[40,64,128]{2,1,0:T(8,128)}), f32[160,64,128]{2,1,0:T(8,128)}) %all-gather.14.cloned.1.call-update) | async-done | bytes 5242896 | tf_op jit(solution)/shard_map/all_gather | solution.py:29
  279.2 4.0 bitcast_add_fusion.7
  283.2 57.7 %all-gather.10.cloned.1.call-done = f32[4,40,64,128]{3,2,1,0:T(8,128)} async-done(((f32[1,40,64,128]{3,2,1,0:T(8,128)}), f32[4,40,64,128]{3,2,1,0:T(8,128)}) %all-gather.10.cloned.1.call-update) | async-done | bytes 5242896 | tf_op jit(solution)/shard_map/all_gather | solution.py:29
  341.0 4.0 multiply_add_fusion.1
  345.6 7.7 %all-gather.4 = f32[4,1,40]{2,1,0:T(1,128)S(1)} all-gather(f32[1,1,40]{2,1,0:T(1,128)S(1)} %get-tuple-element.39), channel_id=1, replica_groups=mesh['seq_0'=4,'seq_1'=4,'seq_2'=4,'fsdp'=2] {'seq_0'}, dimensions={0}, use_global_device_ids=true | all-gather | bytes 800 | tf_op jit(solution)/shard_map/all_gather | solution.py:29
  353.9 1.1 fusion.87
  355.0 1.1 fusion.90
  356.1 1.1 fusion.97
  357.2 45.2 %all-gather.12.cloned.1.call-done = f32[4,40,64,128]{3,2,1,0:T(8,128)} async-done(((f32[1,40,64,128]{3,2,1,0:T(8,128)}), f32[4,40,64,128]{3,2,1,0:T(8,128)}) %all-gather.12.cloned.1.call-update) | async-done | bytes 5242896 | tf_op jit(solution)/shard_map/all_gather | solution.py:29
  402.4 8.0 %fusion.60 = f32[40,64,128]{2,1,0:T(8,128)S(1)} fusion(f32[4,40,64,128]{3,2,1,0:T(8,128)} %all-gather.12.cloned.1.call-done, f32[4,40,64,128]{3,2,1,0:T(8,128)} %all-gather.10.cloned.1.call-done, f32[160,64,128]{2,1,0:T(8,128)} %all-gather.14.cloned.1.call-done, f32[40]{0:T(128)} %copy-done.17, f32[40]{0:T(128)S(1)} %get-tuple-element.47, f32[40]{0:T(128)} %copy-done.18, ...), kind=kLoop, calls=%fused_computation.75 | loop fusion | flops 12124160 | bytes 17041612 | tf_op jit(solution)/shard_map/add | solution.py:68
  410.5 1.7 fusion.70
  412.2 1.7 fusion.77
  414.0 1.8 fusion.84
  415.8 5.2 %fusion.49 = f32[256,40,64]{0,2,1:T(8,128)S(1)} fusion(bf16[256,40,64]{0,2,1:T(8,128)(2,1)S(1)} %bitcast.222, f32[256,40,64]{0,2,1:T(8,128)S(1)} %fusion.70, f32[40,256]{1,0:T(8,128)S(1)} %copy-done.14, f32[40,256]{1,0:T(8,128)S(1)} %copy_bitcast_fusion, f32[256,256]{1,0:T(8,128)S(1)} %fusion.87, pred[256,256]{1,0:T(8,128)(4,1)S(1)} %copy-done.8, ...), kind=kOutput, calls=%fused_computation.66 | convolution fusion | flops 1020395520 | bytes 7004320 | tf_op jit(solution)/shard_map/hij,jhp->ihp/dot_general | solution.py:48
  421.1 5.5 %fusion.47 = f32[256,40,64]{0,2,1:T(8,128)S(1)} fusion(bf16[256,40,64]{0,2,1:T(8,128)(2,1)S(1)} %bitcast.220, f32[256,40,64]{0,2,1:T(8,128)S(1)} %fusion.77, f32[40,256]{1,0:T(8,128)S(1)} %copy-done.13, f32[40,256]{1,0:T(8,128)S(1)} %copy_bitcast_fusion.1, f32[256,256]{1,0:T(8,128)S(1)} %fusion.90, pred[256,256]{1,0:T(8,128)(4,1)S(1)} %copy-done.8, ...), kind=kOutput, calls=%fused_computation.64 | convolution fusion | flops 1020395520 | bytes 7004320 | tf_op jit(solution)/shard_map/hij,jhp->ihp/dot_general | solution.py:48
  426.6 5.2 %fusion.45 = f32[256,40,64]{0,2,1:T(8,128)S(1)} fusion(bf16[256,40,64]{0,2,1:T(8,128)(2,1)S(1)} %bitcast.218, f32[256,40,64]{0,2,1:T(8,128)S(1)} %fusion.84, f32[40,256]{1,0:T(8,128)S(1)} %copy-done.12, f32[40,256]{1,0:T(8,128)S(1)} %copy_bitcast_fusion.2, f32[256,256]{1,0:T(8,128)S(1)} %fusion.97, pred[256,256]{1,0:T(8,128)(4,1)S(1)} %copy-done.8, ...), kind=kOutput, calls=%fused_computation.62 | convolution fusion | flops 1020395520 | bytes 7004320 | tf_op jit(solution)/shard_map/hij,jhp->ihp/dot_general | solution.py:48
  431.8 4.4 multiply_reduce_fusion
  436.3 2.6 fusion.42
  439.0 6.3 %copy.50 = bf16[1,768,2560]{2,1,0:T(8,128)(2,1)} copy(bf16[1,768,2560]{1,2,0:T(8,128)(2,1)} %fusion.42) | data formatting | bytes 7864320 | tf_op jit(solution)/shard_map/broadcast_in_dim | solution.py:144
  (103 shorter events, 12.8 us)
Async XLA Ops:
  6.5 113.8 %all-gather.16.cloned.1.call-start = ((), (), s32[]{:S(2)}) async-start(), calls=%async_computation.3 | async-start | bytes 34080768 | tf_op jit(solution)/shard_map/all_gather | solution.py:85
  7.3 271.9 %all-gather.14.cloned.1.call-start = ((), (), s32[]{:S(2)}) async-start(), calls=%async_computation.2 | async-start | bytes 6553600 | tf_op jit(solution)/shard_map/all_gather | solution.py:29
  10.0 184.6 %copy-start.19 = (pred[768]{0:T(1024)(128)(4,1)}, pred[768]{0:T(1024)(128)(4,1)S(1)}, u32[]{:S(2)}) copy-start(pred[768]{0:T(1024)(128)(4,1)S(1)} %iota_compare_fusion.1) | copy-start | bytes 2308
  186.2 8.4 %copy-start.24 = (f32[40]{0:T(128)S(1)}, f32[40]{0:T(128)}, u32[]{:S(2)}) copy-start(f32[40]{0:T(128)} %param.14) | copy-start | bytes 484
  186.2 9.4 %copy-start.25 = (f32[40]{0:T(128)S(1)}, f32[40]{0:T(128)}, u32[]{:S(2)}) copy-start(f32[40]{0:T(128)} %param.15) | copy-start | bytes 484
  188.8 2.0 copy-start
  190.8 10.2 %copy-start.15 = (f32[2816]{0:T(1024)S(1)}, f32[2816]{0:T(1024)}, u32[]{:S(2)}) copy-start(f32[2816]{0:T(1024)} %param.13) | copy-start | bytes 33796
  191.3 9.2 %collective-permute-start = (bf16[3,2816]{1,0:T(4,128)(2,1)S(1)}, bf16[3,2816]{1,0:T(4,128)(2,1)S(1)}, u32[]{:S(2)}, u32[]{:S(2)}) collective-permute-start(bf16[3,2816]{1,0:T(4,128)(2,1)S(1)} %copy.36), channel_id=1, source_target_pairs={{0,2},{2,4},{4,6},{6,8},{8,10},{10,12},{12,14},{14,16},{16,18},{18... | collective-permute-start | bytes 50696 | tf_op jit(solution)/shard_map/ppermute | solution.py:15
  200.5 18.5 %copy-start.22 = (f32[40]{0:T(128)}, f32[40]{0:T(128)S(1)}, u32[]{:S(2)}) copy-start(f32[40]{0:T(128)S(1)} %exp.98) | copy-start | bytes 484
  217.0 2.9 copy-start.1
  217.3 1.8 copy-start.4
  217.3 3.0 copy-start.6
  220.3 2.0 copy-start.27
  222.2 118.8 %all-gather.10.cloned.1.call-start = ((), (), s32[]{:S(2)}) async-start(), calls=%async_computation | async-start | bytes 6553600 | tf_op jit(solution)/shard_map/all_gather | solution.py:29
  240.8 42.4 %copy-start.17 = (f32[40]{0:T(128)}, f32[40]{0:T(128)S(1)}, u32[]{:S(2)}) copy-start(f32[40]{0:T(128)S(1)} %get-tuple-element.44) | copy-start | bytes 484
  240.8 42.4 %copy-start.18 = (f32[40]{0:T(128)}, f32[40]{0:T(128)S(1)}, u32[]{:S(2)}) copy-start(f32[40]{0:T(128)S(1)} %get-tuple-element.45) | copy-start | bytes 484
  283.2 119.2 %all-gather.12.cloned.1.call-start = ((), (), s32[]{:S(2)}) async-start(), calls=%async_computation.1 | async-start | bytes 6553600 | tf_op jit(solution)/shard_map/all_gather | solution.py:29
  402.4 8.0 %copy-start.21 = (f32[40]{0:T(128)S(1)}, f32[40]{0:T(128)}, u32[]{:S(2)}) copy-start(f32[40]{0:T(128)} %get-tuple-element.49) | copy-start | bytes 484
  402.4 8.0 %copy-start.23 = (f32[40]{0:T(128)S(1)}, f32[40]{0:T(128)}, u32[]{:S(2)}) copy-start(f32[40]{0:T(128)} %copy-done.22) | copy-start | bytes 484
  413.9 1.8 copy-start.7
  413.9 1.8 copy-start.8
  413.9 1.8 copy-start.11
  414.0 1.8 copy-start.14
  414.0 1.8 copy-start.26
  415.8 5.3 %copy-start.5 = (bf16[256,2560]{0,1:T(8,128)(2,1)S(1)}, bf16[256,2560]{0,1:T(8,128)(2,1)}, u32[]{:S(2)}) copy-start(bf16[256,2560]{0,1:T(8,128)(2,1)} %copy-done.4) | copy-start | bytes 3932164
  415.8 5.2 %copy-start.10 = (f32[256,40]{0,1:T(8,128)S(1)}, f32[256,40]{0,1:T(8,128)}, u32[]{:S(2)}) copy-start(f32[256,40]{0,1:T(8,128)} %get-tuple-element.33) | copy-start | bytes 122884
  415.8 5.2 %copy-start.13 = (f32[40,256]{1,0:T(8,128)S(1)}, f32[40,256]{1,0:T(8,128)}, u32[]{:S(2)}) copy-start(f32[40,256]{1,0:T(8,128)} %get-tuple-element.24) | copy-start | bytes 122884
  421.1 5.5 %copy-start.3 = (bf16[256,2560]{0,1:T(8,128)(2,1)S(1)}, bf16[256,2560]{0,1:T(8,128)(2,1)}, u32[]{:S(2)}) copy-start(bf16[256,2560]{0,1:T(8,128)(2,1)} %copy-done.2) | copy-start | bytes 3932164
  421.1 5.5 %copy-start.9 = (f32[256,40]{0,1:T(8,128)S(1)}, f32[256,40]{0,1:T(8,128)}, u32[]{:S(2)}) copy-start(f32[256,40]{0,1:T(8,128)} %get-tuple-element.32) | copy-start | bytes 122884
  421.1 5.5 %copy-start.12 = (f32[40,256]{1,0:T(8,128)S(1)}, f32[40,256]{1,0:T(8,128)}, u32[]{:S(2)}) copy-start(f32[40,256]{1,0:T(8,128)} %get-tuple-element.23) | copy-start | bytes 122884
  431.8 4.5 copy-start.16
  431.8 4.5 copy-start.20
  (1 other events, 1.8 us)
Sparse Core Ops, SparseCore 0:
  10.3 110.0 all-gather.15
  222.3 56.7 all-gather.13
  283.3 57.6 all-gather.9
  345.1 57.2 all-gather.11
where the time goes:
time: 460 us; the launch traced here: 452 us
  waiting for transfers between devices  251 us (55%)
  matrix products  57 us (12%)
  local copies, waits for them, and re-layouts  54 us (12%)
  other arithmetic  46.4 us (10%)
  blocking collectives  24.1 us (5%)
  between operations  15.9 us (3%)
    all_gather x3, waiting for transfers between devices, prefix_by_axis(): pieces = jax.tree.map(lambda part: lax.all_gather(part, axis), total)  141 us
    all_gather x1, waiting for transfers between devices, local(): lax.all_gather(in_weight, SEQ_FSDP, axis=0, tiled=True)  109 us
    unnamed x60, local copies, waits for them, and re-layouts  41 us
    dot_general x1, matrix products, local(): jnp.dot(own_rows, lax.all_gather(in_weight, SEQ_FSDP, axis=0, tiled=True)...  29 us
    all_gather x2, blocking collectives, prefix_by_axis(): pieces = jax.tree.map(lambda part: lax.all_gather(part, axis), total)  16.3 us
    convert_element_type x1, other arithmetic, local(): conv_out = jax.nn.silu(convolved).astype(jnp.bfloat16)  16 us
    add x3, other arithmetic, compose(): later[0][:, None, None] * earlier[1] + later[1]  16 us
    dot_general x3, matrix products, block_terms(): jnp.einsum('hij,jhp->ihp', mixing, head_input, precision=lax.Precision.HIGH)  15.9 us
  transfers between devices with their start and end apart: 5, of which 4 were waited for; matrix products, arithmetic and copies ran while one was open for 3% of the time, Pallas kernels for 0%

commit v1 on v0

v1 whole, which is shorter than its diff:
```python
import functools

import jax
import jax.numpy as jnp
from jax import lax
from jax.experimental import pallas as pl
from jax.experimental.pallas import tpu as pltpu
from jax.sharding import Mesh
from jax.sharding import PartitionSpec as P

BLOCK = 256
CHUNK = 128
HALO = 16
LANES = 128
LOG2E = 1.4426950408889634
AXES = ("y", "z", "xh", "xl")
F32 = jnp.float32
BF16 = jnp.bfloat16
MESH = pl.DeviceIdType.MESH
ORDERS = (("x", "y", "z"), ("y", "z", "x"), ("z", "x", "y"))


def split3(value):
    hi = value.astype(BF16)
    rest = value - hi.astype(F32)
    mid = rest.astype(BF16)
    lo = (rest - mid.astype(F32)).astype(BF16)
    return hi, mid, lo


def split2(value):
    hi = value.astype(BF16)
    lo = (value - hi.astype(F32)).astype(BF16)
    return hi, lo


def dot(a, b):
    return jnp.dot(a, b, preferred_element_type=F32)


def place():
    return {
        "y": lax.axis_index("y"),
        "z": lax.axis_index("z"),
        "x": lax.axis_index("xh") * 2 + lax.axis_index("xl"),
    }


def device_of(axis, coordinate):
    if axis == "x":
        return {"xh": coordinate // 2, "xl": lax.rem(coordinate, 2)}
    return {axis: coordinate}


def gather_kernel(block_ref, out_ref, local_sem, send_sem, recv_sem):
    me = place()
    near = lambda axis, step: lax.rem(me[axis] + step + 4, 4)
    barrier = pltpu.get_barrier_semaphore()
    for axis in ("y", "z", "x"):
        for step in (1, -1):
            pl.semaphore_signal(
                barrier, inc=1, device_id=device_of(axis, near(axis, step)), device_id_type=MESH
            )
    pl.semaphore_wait(barrier, 6)
    width = block_ref.shape[1] // 6

    def region(color, half, where):
        y, z, x = (where[axis] for axis in ("y", "z", "x"))
        xl, xh = (slice(None), slice(None)) if x is None else (lax.rem(x, 2), x // 2)
        y = slice(None) if y is None else y
        z = slice(None) if z is None else z
        return out_ref.at[xl, y, z, xh, :, pl.ds((color * 2 + half) * width, width)]

    own = pltpu.make_async_copy(
        block_ref, out_ref.at[lax.rem(me["x"], 2), me["y"], me["z"], me["x"] // 2], local_sem
    )
    own.start()

    def where(color, stage, coordinate):
        order = ORDERS[color]
        spot = dict(me)
        for axis in order[:stage]:
            spot[axis] = None
        spot[order[stage]] = coordinate
        return spot

    SLOTS = ((0, 0, 1), (0, 1, 1), (-1, 0, 1), (0, 1, -1), (0, 0, -1), (1, 1, -1))

    def copy(color, stage, slot):
        offset, half, step = SLOTS[slot]
        axis = ORDERS[color][stage]
        target = region(color, half, where(color, stage, near(axis, offset)))
        source = target
        if stage == 0 and offset == 0:
            source = block_ref.at[:, pl.ds((color * 2 + half) * width, width)]
        return pltpu.make_async_remote_copy(
            src_ref=source,
            dst_ref=target,
            send_sem=send_sem.at[color, stage, slot],
            recv_sem=recv_sem.at[color, stage, slot],
            device_id=device_of(axis, near(axis, step)),
            device_id_type=MESH,
        )

    def arrival(color, stage, slot):
        offset, half, step = SLOTS[slot]
        axis = ORDERS[color][stage]
        target = region(color, half, where(color, stage, near(axis, offset - step)))
        return pltpu.make_async_remote_copy(
            src_ref=target,
            dst_ref=target,
            send_sem=send_sem.at[color, stage, slot],
            recv_sem=recv_sem.at[color, stage, slot],
            device_id=device_of(axis, near(axis, step)),
            device_id_type=MESH,
        )

    for stage in range(3):
        for color in range(3):
            if stage:
                for slot in (1, 2, 4, 5):
                    arrival(color, stage - 1, slot).wait_recv()
                if stage == 1 and color == 0:
                    own.wait()
            for slot in (0, 3, 1, 4):
                copy(color, stage, slot).start()
        for color in range(3):
            arrival(color, stage, 0).wait_recv()
            copy(color, stage, 2).start()
            arrival(color, stage, 3).wait_recv()
            copy(color, stage, 5).start()
    for color in range(3):
        for slot in (1, 2, 4, 5):
            arrival(color, 2, slot).wait_recv()
    for stage in range(3):
        for color in range(3):
            for slot in range(6):
                copy(color, stage, slot).wait_send()


def gather_weight(block):
    rows, columns = block.shape
    return pl.pallas_call(
        gather_kernel,
        out_shape=jax.ShapeDtypeStruct((2, 4, 4, 2, rows, columns), BF16),
        in_specs=[pl.BlockSpec(memory_space=pltpu.VMEM)],
        out_specs=pl.BlockSpec(memory_space=pl.ANY),
        scratch_shapes=[
            pltpu.SemaphoreType.DMA,
            pltpu.SemaphoreType.DMA((3, 3, 6)),
            pltpu.SemaphoreType.DMA((3, 3, 6)),
        ],
        compiler_params=pltpu.CompilerParams(collective_id=0, has_side_effects=True),
        name="weight_gather",
    )(block)


def scan_kernel(
    live_ref, mixed_ref, raw_ref, taps_ref, bias_ref, dt_ref, decay_ref, skip_ref, spread_ref,
    tri_ref, y_ref, map_ref, cum_ref, state_ref, total_ref,
):
    inner = skip_ref.shape[1]
    state_width = (mixed_ref.shape[2] - inner) // 2
    chunk = pl.program_id(1)
    row0 = pl.multiple_of(chunk * CHUNK, CHUNK)

    @pl.when(chunk == 0)
    def _():
        state_ref[...] = jnp.zeros_like(state_ref)
        total_ref[...] = jnp.zeros_like(total_ref)

    mixed = mixed_ref[0, pl.ds(row0, CHUNK + HALO), :].astype(F32)
    taps = taps_ref.shape[0]
    conv = bias_ref[...] + taps_ref[0:1, :] * mixed[HALO - taps + 1 : HALO - taps + 1 + CHUNK]
    for k in range(1, taps):
        start = HALO - taps + 1 + k
        conv = conv + taps_ref[k : k + 1, :] * mixed[start : start + CHUNK]
    act = (conv * jax.nn.sigmoid(conv)).astype(BF16)
    x = act[:, :inner]
    in_map = act[:, inner : inner + state_width]
    out_map = act[:, inner + state_width :]

    raw = raw_ref[0, pl.ds(row0 + HALO, CHUNK), :].astype(F32) + dt_ref[...]
    tail = jnp.exp(-jnp.abs(raw))
    log1p = jnp.where(
        tail < 0.01, tail * (1.0 - tail * (0.5 - tail * (1.0 / 3.0 - 0.25 * tail))), jnp.log(1.0 + tail)
    )
    step = jnp.maximum(raw, 0.0) + log1p
    rows = lax.broadcasted_iota(jnp.int32, (CHUNK, LANES), 0)
    columns = lax.broadcasted_iota(jnp.int32, (CHUNK, LANES), 1)
    step = jnp.where(rows + row0 < live_ref[pl.program_id(0)], step, 0.0)
    log_decay = -(step * decay_ref[...]) * LOG2E
    cum = dot(tri_ref[...], jnp.concatenate(split3(log_decay), axis=0))
    shifted = jnp.where(step > 0.0, cum - jnp.log(step) * LOG2E, 1e30).T
    causal = rows >= columns
    scores = lax.dot_general(out_map, in_map, (((1,), (1,)), ((), ())), preferred_element_type=F32)

    state = state_ref[0]
    growth = dot(jnp.concatenate(split3(jnp.exp2(cum)), axis=1), spread_ref[...])
    reach = dot(
        jnp.concatenate([out_map, out_map], axis=1), jnp.concatenate(split2(state), axis=0)
    )
    base = growth * reach + skip_ref[...] * x.astype(F32)
    left = columns < LANES // 2
    zero = jnp.zeros((CHUNK, LANES), BF16)
    for tile in range(inner // LANES):
        lanes = slice(tile * LANES, (tile + 1) * LANES)
        total = base[:, lanes]
        for part in range(2):
            head = tile * 2 + part
            reached = jnp.where(
                causal, cum[:, head : head + 1] - shifted[head : head + 1, :], -1e30
            )
            mixing = jnp.exp2(reached) * scores
            values = jnp.where(left if part == 0 else ~left, x[:, lanes], zero)
            total = total + dot(
                jnp.concatenate(split2(mixing), axis=1), jnp.concatenate([values, values], axis=0)
            )
        y_ref[0, :, lanes] = total

    last = cum[CHUNK - 1 : CHUNK, :]
    to_end = jnp.exp2(last - cum) * step
    weighted = x.astype(F32) * dot(jnp.concatenate(split3(to_end), axis=1), spread_ref[...])
    added = lax.dot_general(
        jnp.concatenate([in_map, in_map], axis=0),
        jnp.concatenate(split2(weighted), axis=0),
        (((0,), (0,)), ((), ())),
        preferred_element_type=F32,
    )
    state_ref[0] = growth[CHUNK - 1 : CHUNK, :] * state + added
    map_ref[0] = out_map
    cum_ref[0] = cum + total_ref[0]
    total_ref[0] = total_ref[0] + last


def scan_call(live, mixed, raw, taps, bias, dt, decay, skip, spread, tri):
    seqs, padded, width = mixed.shape
    slots = padded - HALO
    inner = skip.shape[1]
    state_width = (width - inner) // 2
    chunks = slots // CHUNK
    whole = lambda a: pl.BlockSpec(a.shape, lambda q, c: (0,) * a.ndim)
    return pl.pallas_call(
        scan_kernel,
        grid=(seqs, chunks),
        in_specs=[
            pl.BlockSpec(memory_space=pltpu.SMEM),
            pl.BlockSpec((1, padded, width), lambda q, c: (q, 0, 0)),
            pl.BlockSpec((1, padded, LANES), lambda q, c: (q, 0, 0)),
            whole(taps), whole(bias), whole(dt), whole(decay), whole(skip), whole(spread), whole(tri),
        ],
        out_specs=[
            pl.BlockSpec((1, CHUNK, inner), lambda q, c: (q, c, 0)),
            pl.BlockSpec((1, CHUNK, state_width), lambda q, c: (q, c, 0)),
            pl.BlockSpec((1, CHUNK, LANES), lambda q, c: (q, c, 0)),
            pl.BlockSpec((1, state_width, inner), lambda q, c: (q, 0, 0)),
            pl.BlockSpec((1, 1, LANES), lambda q, c: (q, 0, 0)),
        ],
        out_shape=[
            jax.ShapeDtypeStruct((seqs, slots, inner), F32),
            jax.ShapeDtypeStruct((seqs, slots, state_width), BF16),
            jax.ShapeDtypeStruct((seqs, slots, LANES), F32),
            jax.ShapeDtypeStruct((seqs, state_width, inner), F32),
            jax.ShapeDtypeStruct((seqs, 1, LANES), F32),
        ],
        compiler_params=pltpu.CompilerParams(
            dimension_semantics=("arbitrary", "arbitrary"), vmem_limit_bytes=50 * 1024 * 1024
        ),
        name="conv_scan",
    )(live, mixed, raw, taps, bias, dt, decay, skip, spread, tri)


def prefix_kernel(
    state_ref, total_ref, spread_ref, in_ref, decays, pieces, arrived, starts, factors,
    send_sem, recv_sem, dsend_sem, drecv_sem, bsend_sem, brecv_sem,
):
    count = 64
    y, z, xh, xl = (lax.axis_index(axis) for axis in AXES)
    me = ((y * 4 + z) * 2 + xh) * 2 + xl
    inner = state_ref.shape[2]
    wide = inner // 2

    def device(index):
        return {
            "y": index // 16,
            "z": lax.rem(index // 4, 4),
            "xh": lax.rem(index // 2, 2),
            "xl": lax.rem(index, 2),
        }

    def slice_of(ref, index):
        row = pl.multiple_of(lax.rem(index // 2, 16) * 8, 8)
        column = pl.multiple_of(lax.rem(index, 2) * wide, LANES)
        return ref.at[index // 32, pl.ds(row, 8), pl.ds(column, wide)]

    barrier = pltpu.get_barrier_semaphore()

    @pl.loop(1, count)
    def _(i):
        pl.semaphore_signal(
            barrier, inc=1, device_id=device(lax.rem(me + i, count)), device_id_type=MESH
        )

    pl.semaphore_wait(barrier, count - 1)
    decays[...] = jnp.exp2(total_ref[...])

    def piece(index, slot):
        return pltpu.make_async_remote_copy(
            src_ref=slice_of(state_ref, index), dst_ref=arrived.at[slot],
            send_sem=send_sem.at[index], recv_sem=recv_sem.at[slot],
            device_id=device(index), device_id_type=MESH,
        )

    def factor(index, slot):
        return pltpu.make_async_remote_copy(
            src_ref=total_ref.at[index // 32], dst_ref=pieces.at[slot],
            send_sem=dsend_sem.at[index], recv_sem=drecv_sem.at[slot],
            device_id=device(index), device_id_type=MESH,
        )

    def back(index, slot):
        return pltpu.make_async_remote_copy(
            src_ref=starts.at[index], dst_ref=slice_of(in_ref, slot),
            send_sem=bsend_sem.at[index], recv_sem=brecv_sem.at[slot],
            device_id=device(index), device_id_type=MESH,
        )

    @pl.loop(1, count)
    def _(i):
        peer = lax.rem(me + i, count)
        factor(peer, me).start()
        piece(peer, me).start()

    arrived[me] = slice_of(state_ref, me)[...]
    pieces[me] = total_ref[me // 32]

    @pl.loop(1, count)
    def _(i):
        peer = lax.rem(me + i, count)
        factor(peer, peer).wait_recv()

    column = pl.multiple_of(lax.rem(me, 2) * wide, LANES)
    decay = jnp.exp2(pieces[...].reshape(count, LANES))
    factors[...] = dot(
        jnp.concatenate(split3(decay), axis=1), spread_ref[:, pl.ds(column, wide)]
    )

    @pl.loop(1, count)
    def _(i):
        peer = lax.rem(me + i, count)
        piece(peer, peer).wait_recv()

    def compose(index, carry):
        starts[index] = carry
        return factors[pl.ds(index, 1), :] * carry + arrived[index]

    lax.fori_loop(0, count, compose, jnp.zeros((8, wide), F32))

    @pl.loop(1, count)
    def _(i):
        back(lax.rem(me + i, count), me).start()

    slice_of(in_ref, me)[...] = starts[me]

    @pl.loop(1, count)
    def _(i):
        peer = lax.rem(me + i, count)
        back(peer, peer).wait_recv()

    @pl.loop(1, count)
    def _(i):
        peer = lax.rem(me + i, count)
        piece(peer, me).wait_send()
        factor(peer, me).wait_send()
        back(peer, me).wait_send()


def prefix_call(state, total, spread):
    seqs, state_width, inner = state.shape
    wide = inner // 2
    return pl.pallas_call(
        prefix_kernel,
        out_shape=jax.ShapeDtypeStruct(state.shape, F32),
        in_specs=[pl.BlockSpec(memory_space=pltpu.VMEM)] * 3,
        out_specs=pl.BlockSpec(memory_space=pltpu.VMEM),
        scratch_shapes=[
            pltpu.VMEM((seqs, 1, LANES), F32),
            pltpu.VMEM((64, 1, LANES), F32),
            pltpu.VMEM((64, 8, wide), F32),
            pltpu.VMEM((64, 8, wide), F32),
            pltpu.VMEM((64, wide), F32),
        ]
        + [pltpu.SemaphoreType.DMA((64,))] * 6,
        compiler_params=pltpu.CompilerParams(collective_id=1, has_side_effects=True),
        name="state_prefix",
    )(state, total, spread)


def gated_kernel(y_ref, map_ref, cum_ref, gate_ref, start_ref, spread_ref, out_ref, square_ref):
    growth = dot(jnp.concatenate(split3(jnp.exp2(cum_ref[0])), axis=1), spread_ref[...])
    out_map = map_ref[0]
    reach = dot(
        jnp.concatenate([out_map, out_map], axis=1),
        jnp.concatenate(split2(start_ref[0]), axis=0),
    )
    row0 = pl.multiple_of(pl.program_id(1) * CHUNK, CHUNK)
    gate = gate_ref[0, pl.ds(row0 + HALO, CHUNK), :].astype(F32)
    gated = (y_ref[0] + growth * reach) * (gate * jax.nn.sigmoid(gate))
    out_ref[0] = gated
    square_ref[0] = jnp.broadcast_to(jnp.sum(gated * gated, axis=1, keepdims=True), (CHUNK, LANES))


def gated_call(y, out_map, cum, gate, start, spread):
    seqs, slots, inner = y.shape
    state_width = out_map.shape[2]
    padded = gate.shape[1]
    return pl.pallas_call(
        gated_kernel,
        grid=(seqs, slots // CHUNK),
        in_specs=[
            pl.BlockSpec((1, CHUNK, inner), lambda q, c: (q, c, 0)),
            pl.BlockSpec((1, CHUNK, state_width), lambda q, c: (q, c, 0)),
            pl.BlockSpec((1, CHUNK, LANES), lambda q, c: (q, c, 0)),
            pl.BlockSpec((1, padded, inner), lambda q, c: (q, 0, 0)),
            pl.BlockSpec((1, state_width, inner), lambda q, c: (q, 0, 0)),
            pl.BlockSpec(spread.shape, lambda q, c: (0, 0)),
        ],
        out_specs=[
            pl.BlockSpec((1, CHUNK, inner), lambda q, c: (q, c, 0)),
            pl.BlockSpec((1, CHUNK, LANES), lambda q, c: (q, c, 0)),
        ],
        out_shape=[
            jax.ShapeDtypeStruct((seqs, slots, inner), F32),
            jax.ShapeDtypeStruct((seqs, slots, LANES), F32),
        ],
        compiler_params=pltpu.CompilerParams(dimension_semantics=("arbitrary", "arbitrary")),
        name="gated",
    )(y, out_map, cum, gate, start, spread)


def local(
    tokens, bounds, in_weight, conv_weight, conv_bias, dt_bias, decay_rate, skip_gain, norm_gain
):
    slots, model = tokens.shape[1:]
    width = norm_gain.shape[0]
    inner = width // 2
    state_width = (conv_bias.shape[0] - width) // 2
    heads = decay_rate.shape[0] // 2
    core = lax.axis_index("core")
    swap = [(0, 1), (1, 0)]

    def half(array, start, size):
        low = array[..., start : start + size]
        return jnp.where(core == 0, low, array[..., start + size : start + 2 * size])

    rows = lax.all_gather(in_weight, ("xl", "core"), axis=0, tiled=True)
    first = jnp.concatenate(
        [half(rows, width, inner), rows[:, 2 * width : 2 * width + 2 * state_width]], axis=1
    )
    raw = half(rows, 2 * width + 2 * state_width, heads)
    second = jnp.concatenate(
        [
            jnp.pad(raw, ((0, 0), (0, LANES - heads))),
            half(rows, 0, inner),
            jnp.zeros((rows.shape[0], first.shape[1] - inner - LANES), BF16),
        ],
        axis=1,
    )
    block = jnp.where(lax.axis_index("xl") == 0, first, second)
    weight = gather_weight(block).reshape(2, model, first.shape[1])

    blocks = bounds[0, 0, 1] - bounds[0, 0, 0]
    edge = lax.dynamic_slice_in_dim(tokens[0], blocks * BLOCK - HALO, HALO, 0)
    edge = lax.ppermute(edge, AXES, [(s, s + 1) for s in range(63)])
    mark = jnp.where(jnp.arange(HALO)[:, None] == 0, blocks.astype(BF16), edge)
    extended = jnp.concatenate([mark, tokens[0]], axis=0)
    other = lax.ppermute(extended, "core", swap)
    live = jnp.stack([blocks, other[0, 0].astype(jnp.int32)]) * BLOCK
    rows_in = jnp.concatenate([extended, other], axis=0)
    mixed = dot(rows_in, weight[0]).astype(BF16).reshape(2, slots + HALO, -1)
    rest = dot(rows_in, weight[1]).astype(BF16).reshape(2, slots + HALO, -1)

    spread = (jnp.arange(inner)[None, :] // (inner // heads) == jnp.arange(LANES)[:, None]).astype(BF16)
    spread = jnp.concatenate([spread] * 3, axis=0)
    tri = (jnp.arange(CHUNK)[:, None] >= jnp.arange(CHUNK)[None, :]).astype(BF16)
    tri = jnp.concatenate([tri] * 3, axis=1)
    own_columns = lambda a: jnp.concatenate([half(a, 0, inner), a[..., width:]], axis=-1)
    per_head = lambda a: jnp.pad(half(a, 0, heads), (0, LANES - heads))[None]
    skip = jnp.repeat(half(skip_gain, 0, heads), inner // heads)[None]
    y, out_map, cum, state, total = scan_call(
        live, mixed, rest[:, :, :LANES], own_columns(conv_weight), own_columns(conv_bias)[None],
        per_head(dt_bias), per_head(decay_rate), skip, spread, tri,
    )
    start = prefix_call(state, total, spread)
    gated, square = gated_call(y, out_map, cum, rest[:, :, LANES : LANES + inner], start, spread)
    square = square[:, :, :1]
    square = square + lax.ppermute(square[::-1], "core", swap)
    normed = gated * lax.rsqrt(square / width + 1e-05) * half(norm_gain, 0, inner)[None, None]
    normed = normed.astype(BF16)
    far = lax.ppermute(normed[1], "core", swap)
    near = normed[0]
    out = jnp.where(
        core == 0, jnp.concatenate([near, far], axis=1), jnp.concatenate([far, near], axis=1)
    )
    out = jnp.where(jnp.arange(slots)[:, None] < live[0], out, jnp.zeros_like(out))
    return out[None]


def solution(mesh):
    split = Mesh(mesh.devices.reshape(4, 4, 2, 2, 2), AXES + ("core",))
    return jax.shard_map(
        local,
        mesh=split,
        in_specs=(
            P("core", AXES, None),
            P("core", AXES, None),
            P(AXES + ("core",), None),
            P(), P(), P(), P(), P(), P(),
        ),
        out_specs=P("core", AXES, None),
        check_vma=False,
    )
```

time: 460 us -> 257 us (0.56); the launches traced: 452 us -> 256 us
  waiting for transfers between devices: 251 us -> 4.41 us
  Pallas kernels: 0 us -> 159 us
  other arithmetic: 46.4 us -> 14.4 us
  local copies, waits for them, and re-layouts: 54 us -> 23.7 us
  matrix products: 57 us -> 35.1 us
  between operations: 15.9 us -> 2.25 us
  blocking collectives: 24.1 us -> 11.1 us
    all_gather x4 -> x0, waiting for transfers between devices: 251 us -> none  [the longest x3 141 us: prefix_by_axis(): pieces = jax.tree.map(lambda part: lax.all_gather(part, axis), total)]
    pallas_call x0 -> x4, Pallas kernels: none -> 159 us  [the longest x1 66.5 us: gather_weight(): pl.pallas_call(gather_kernel, out_shape=jax.ShapeDtypeStruct((2, 4, 4, 2,...]
    unnamed x60 -> x23, local copies, waits for them, and re-layouts: 41 us -> 3.65 us
    dot_general x13 -> x2, matrix products: 57 us -> 35.1 us  [dot(): return jnp.dot(a, b, preferred_element_type=F32)]
    add x3 -> x0, other arithmetic: 16 us -> none  [compose(): later[0][:, None, None] * earlier[1] + later[1]]
    convert_element_type x1, other arithmetic: 16 us -> 3.95 us  [local(): normed = normed.astype(BF16)]
    slice x5 -> x10, local copies, waits for them, and re-layouts: 5.39 us -> 17.3 us  [the longest x1 9.18 us: local(): rest = dot(rows_in, weight[1]).astype(BF16).reshape(2, slots + HALO, -1)]
    unnamed x1 -> x0, blocking collectives: 7.71 us -> none
  transfers between devices with their start and end apart: 5 -> 4, of which waited for: 4 -> 2; matrix products, arithmetic and copies ran while one was open for 3% -> 4% of each run, Pallas kernels for 0% -> 26%
where the time goes in v1:
time: 257 us; the launch traced here: 256 us
  Pallas kernels  159 us (62%)
  matrix products  35.1 us (14%)
  local copies, waits for them, and re-layouts  23.7 us (9%)
  other arithmetic  14.4 us (6%)
  blocking collectives  11.1 us (4%)
  starting transfers between devices  6.54 us (3%)
  waiting for transfers between devices  4.41 us (2%)
    pallas_call x1, Pallas kernels, gather_weight(): pl.pallas_call(gather_kernel, out_shape=jax.ShapeDtypeStruct((2, 4, 4, 2,...  66.5 us
    pallas_call x1, Pallas kernels, prefix_call(): pl.pallas_call(prefix_kernel, out_shape=jax.ShapeDtypeStruct(state.shape,...  47.1 us
    dot_general x2, matrix products, dot(): return jnp.dot(a, b, preferred_element_type=F32)  35.1 us
    pallas_call x1, Pallas kernels, scan_call(): pl.pallas_call(scan_kernel, grid=(seqs, chunks), in_specs=[pl.BlockSpec(m...  30.2 us
    pallas_call x1, Pallas kernels, gated_call(): pl.pallas_call(gated_kernel, grid=(seqs, slots // CHUNK), in_specs=[pl.Bl...  14.7 us
    all_gather x1, blocking collectives, local(): rows = lax.all_gather(in_weight, ('xl', 'core'), axis=0, tiled=True)  11.1 us
    slice x1, local copies, waits for them, and re-layouts, local(): rest = dot(rows_in, weight[1]).astype(BF16).reshape(2, slots + HALO, -1)  9.18 us
  transfers between devices with their start and end apart: 4, of which 2 were waited for; matrix products, arithmetic and copies ran while one was open for 4% of the time, Pallas kernels for 26%

profile of v1, /device:TPU:1, one launch (start us, length us, event | category | flops | bytes accessed | tf_op | source)
XLA Modules:
  0.0 256.1 jit_solution(8029216618228704257)
XLA Ops:
  0.0 1.3 fusion.12
  2.6 0.9 dynamic-slice_bitcast_fusion
  3.5 3.9 %collective-permute-start = (bf16[16,2560]{1,0:T(8,128)(2,1)S(1)}, bf16[16,2560]{1,0:T(8,128)(2,1)S(1)}, u32[]{:S(2)}, u32[]{:S(2)}) collective-permute-start(bf16[16,2560]{1,0:T(8,128)(2,1)S(1)} %dynamic-slice_bitcast_fusion), channel_id=1, source_target_pairs={{0,2},{2,4},{4,6},{6,8},{8,10},{10,12},{12,14},{14,16},{16,18},{18... | collective-permute-start | bytes 245768 | tf_op jit(solution)/shard_map/ppermute | solution.py:474
  7.4 11.1 %all-gather = bf16[4,20,5416]{2,1,0:T(8,128)(2,1)S(1)} all-gather(bf16[1,20,5416]{2,1,0:T(8,128)(2,1)} %bitcast.37), channel_id=1, replica_groups=mesh['y'=4,'z'=4,'xh'=2,'xl'=2,'core'=2] {'xl','core'}, dimensions={0}, use_global_device_ids=true | all-gather | bytes 1083200 | tf_op jit(solution)/shard_map/all_gather | solution.py:456
  18.5 0.4 reshape.148
  19.2 4.4 %pad_maximum_fusion.1 = bf16[784,2560]{1,0:T(8,128)(2,1)} fusion(bf16[768,2560]{1,0:T(8,128)(2,1)} %bitcast.30, bf16[16,2560]{1,0:T(8,128)(2,1)S(1)} %broadcast_select_fusion), kind=kLoop, calls=%fused_computation.4 | loop fusion | flops 8028160 | bytes 8028160 | tf_op jit(solution)/shard_map/concatenate | solution.py:476
  23.7 0.8 fusion.4.block_ref
  24.5 66.5 %weight_gather.1 = bf16[2,4,4,2,80,1536]{5,4,3,2,1,0:T(8,128)(2,1)} custom-call(bf16[80,1536]{1,0:T(8,128)(2,1)} %fusion.4.block_ref), custom_call_target="tpu_custom_call" | custom-call | tf_op jit(solution)/shard_map/weight_gather/pallas_call | solution.py:143
  91.8 9.2 %fusion.10 = (bf16[1,4,4,2,80,1536]{5,4,3,2,1,0:T(8,128)(2,1)}, bf16[1,4,4,2,80,1536]{5,4,3,2,1,0:T(8,128)(2,1)S(1)}) fusion(bf16[2,4,4,2,80,1536]{5,4,3,2,1,0:T(8,128)(2,1)} %weight_gather.1), kind=kLoop, calls=%fused_computation.45 | loop fusion | bytes 31457280 | tf_op jit(solution)/shard_map/slice | solution.py:481
  101.0 18.7 %convolution_convert_fusion = bf16[1568,1536]{1,0:T(8,128)(2,1)} fusion(bf16[2560,1536]{1,0:T(8,128)(2,1)} %bitcast.28, bf16[784,2560]{1,0:T(8,128)(2,1)} %collective-permute-done.1, bf16[768,2560]{1,0:T(8,128)(2,1)} %bitcast.31, bf16[16,2560]{1,0:T(8,128)(2,1)S(1)} %broadcast_select_fusion), kind=kOutput, calls=%fused_computation.2 | convolution fusion | flops 12357746688 | bytes 20709376 | tf_op jit(solution)/shard_map/dot_general | solution.py:38
  119.7 1.0 slice.138.raw_ref
  120.7 4.3 %slice.139.gate_ref = bf16[2,784,1280]{2,1,0:T(8,128)(2,1)} slice(bf16[2,784,1536]{2,1,0:T(8,128)(2,1)} %bitcast.34), slice={[0:2], [0:784], [128:1408]} | slice | bytes 8028160 | tf_op jit(solution)/shard_map/slice | solution.py:495
  125.0 1.2 slice.130
  126.9 16.4 %convolution_convert_fusion.1 = bf16[1568,1536]{1,0:T(8,128)(2,1)} fusion(bf16[2560,1536]{1,0:T(8,128)(2,1)S(1)} %bitcast.27, bf16[784,2560]{1,0:T(8,128)(2,1)} %collective-permute-done.1, bf16[768,2560]{1,0:T(8,128)(2,1)} %bitcast.32, bf16[16,2560]{1,0:T(8,128)(2,1)S(1)} %broadcast_select_fusion), kind=kOutput, calls=%fused_computation.3 | convolution fusion | flops 12357746688 | bytes 20709376 | tf_op jit(solution)/shard_map/dot_general | solution.py:38
  143.3 30.2 %conv_scan.1 = (f32[2,768,1280]{2,1,0:T(8,128)}, bf16[2,768,128]{2,1,0:T(8,128)(2,1)S(1)}, f32[2,768,128]{2,1,0:T(8,128)S(1)}, f32[2,128,1280]{2,1,0:T(8,128)S(1)}, f32[2,1,128]{2,1,0:T(1,128)S(1)}) custom-call(s32[2]{0:T(128)S(1)} %add_multiply_fusion.live_ref, bf16[2,784,1536]{2,1,0:T(8,128)(2,1)} %bitcast.29, bf16[2,784,128]{2,1,0:T(8,128)(2,1)S(1)} %slice.138.raw_ref, ...), custom_call_target="tpu_custom_call" | custom-call | tf_op jit(solution)/shard_map/conv_scan/pallas_call | solution.py:243
  173.5 1.1 copy-done.1
  174.5 0.9 copy-done.2
  175.4 0.8 copy-done.3
  176.2 0.5 copy-done.4
  176.7 47.1 %state_prefix.1.start_ref = f32[2,128,1280]{2,1,0:T(8,128)} custom-call(f32[2,128,1280]{2,1,0:T(8,128)} %copy-done.1, f32[2,1,128]{2,1,0:T(1,128)} %copy-done.4, bf16[384,1280]{1,0:T(8,128)(2,1)} %copy-done), custom_call_target="tpu_custom_call" | custom-call | tf_op jit(solution)/shard_map/state_prefix/pallas_call | solution.py:381
  223.9 14.7 %gated.1 = (f32[2,768,1280]{2,1,0:T(8,128)}, f32[2,768,128]{2,1,0:T(8,128)}) custom-call(f32[2,768,1280]{2,1,0:T(8,128)} %get-tuple-element.12.y_ref, bf16[2,768,128]{2,1,0:T(8,128)(2,1)} %copy-done.3, f32[2,768,128]{2,1,0:T(8,128)} %copy-done.2, bf16[2,784,1280]{2,1,0:T(8,128)(2,1)} %slice.139.gate_ref, f32[2,128,1280]{2,1,0:T(8,128)} %state_prefix.1.start_ref, ...), custom_call_target="tpu_custom_call" | custom-call | tf_op jit(solution)/shard_map/gated/pallas_call | solution.py:417
  238.6 1.2 rev.3
  239.8 0.3 copy.12
  240.0 2.0 collective-permute-start.2
  242.1 0.8 collective-permute-done.2
  242.9 0.3 copy.13
  243.2 1.4 rsqrt_reduce_fusion
  244.6 3.9 %multiply_convert_fusion = bf16[2,768,1280]{2,1,0:T(8,128)(2,1)S(1)} fusion(f32[2,768,1280]{2,1,0:T(8,128)} %get-tuple-element.17, f32[1280]{0:T(1024)S(1)} %slice_select_fusion.4, f32[2,768]{1,0:T(2,128)S(1)} %rsqrt_reduce_fusion), kind=kLoop, calls=%fused_computation.1 | loop fusion | flops 5898240 | bytes 11807744 | tf_op jit(solution)/shard_map/convert_element_type | solution.py:499
  248.6 0.3 fusion.11
  248.8 0.4 collective-permute-start.3
  249.3 3.6 %collective-permute-done.3 = bf16[768,1280]{1,0:T(8,128)(2,1)S(1)} collective-permute-done((bf16[768,1280]{1,0:T(8,128)(2,1)S(1)}, bf16[768,1280]{1,0:T(8,128)(2,1)S(1)}, u32[]{:S(2)}, u32[]{:S(2)}) %collective-permute-start.3) | collective-permute-done | bytes 1966112 | tf_op jit(solution)/shard_map/ppermute | solution.py:500
  252.9 3.2 %fusion = bf16[1,768,2560]{2,1,0:T(8,128)(2,1)} fusion(bf16[1,768,1280]{2,1,0:T(8,128)(2,1)S(1)} %bitcast.36, bf16[1,768,1280]{2,1,0:T(8,128)(2,1)S(1)} %get-tuple-element.21, pred[768]{0:T(1024)(128)(4,1)S(1)} %iota_compare_fusion.3, pred[]{:T(512)S(6)} %eq.49), kind=kLoop, calls=%fused_computation.6 | loop fusion | flops 19660800 | bytes 7865089 | tf_op jit(solution)/shard_map/jit(_where)/select_n | solution.py:505
  (50 shorter events, 1.1 us)
Async XLA Ops:
  3.5 15.6 %collective-permute-start = (bf16[16,2560]{1,0:T(8,128)(2,1)S(1)}, bf16[16,2560]{1,0:T(8,128)(2,1)S(1)}, u32[]{:S(2)}, u32[]{:S(2)}) collective-permute-start(bf16[16,2560]{1,0:T(8,128)(2,1)S(1)} %dynamic-slice_bitcast_fusion), channel_id=1, source_target_pairs={{0,2},{2,4},{4,6},{6,8},{8,10},{10,12},{12,14},{14,16},{16,18},{18... | collective-permute-start | bytes 245768 | tf_op jit(solution)/shard_map/ppermute | solution.py:474
  23.6 77.4 %collective-permute-start.1 = (bf16[784,2560]{1,0:T(8,128)(2,1)}, bf16[784,2560]{1,0:T(8,128)(2,1)}, u32[]{:S(2)}, u32[]{:S(2)}) collective-permute-start(bf16[784,2560]{1,0:T(8,128)(2,1)} %pad_maximum_fusion.1), channel_id=1, source_target_pairs={{0,1},{1,0},{2,3},{3,2},{4,5},{5,4},{6,7},{7,6},{8,9},{9,8},{10,11... | collective-permute-start | bytes 12042248 | tf_op jit(solution)/shard_map/ppermute | solution.py:477
  24.5 66.6 %copy-start.6 = (f32[2816]{0:T(1024)S(1)}, f32[2816]{0:T(1024)}, u32[]{:S(2)}) copy-start(f32[2816]{0:T(1024)} %param.13) | copy-start | bytes 33796
  24.5 66.7 %copy-start.10 = (f32[40]{0:T(128)S(1)}, f32[40]{0:T(128)}, u32[]{:S(2)}) copy-start(f32[40]{0:T(128)} %param.16) | copy-start | bytes 484
  24.5 66.9 %copy-start.8 = (f32[40]{0:T(128)S(1)}, f32[40]{0:T(128)}, u32[]{:S(2)}) copy-start(f32[40]{0:T(128)} %param.15) | copy-start | bytes 484
  24.5 66.9 %copy-start.9 = (f32[40]{0:T(128)S(1)}, f32[40]{0:T(128)}, u32[]{:S(2)}) copy-start(f32[40]{0:T(128)} %param.14) | copy-start | bytes 484
  24.5 67.0 %copy-start.5 = (f32[4,2816]{1,0:T(4,128)S(1)}, f32[4,2816]{1,0:T(4,128)}, u32[]{:S(2)}) copy-start(f32[4,2816]{1,0:T(4,128)} %param.12) | copy-start | bytes 135172
  24.5 67.0 %slice-start = ((f32[4,2816]{1,0:T(4,128)}), f32[4,256]{1,0:T(4,128)S(1)}, s32[]{:S(2)}) async-start(f32[4,2816]{1,0:T(4,128)} %param.12), calls=%async_computation | async-start | bytes 8192 | tf_op jit(solution)/shard_map/slice | solution.py:487
  91.8 51.5 %copy-start = (bf16[384,1280]{1,0:T(8,128)(2,1)}, bf16[384,1280]{1,0:T(8,128)(2,1)S(1)}, u32[]{:S(2)}) copy-start(bf16[384,1280]{1,0:T(8,128)(2,1)S(1)} %add_convert_fusion.spread_ref) | copy-start | bytes 2949124
  173.5 1.1 copy-start.1
  174.5 0.9 copy-start.2
  175.4 0.8 copy-start.3
  176.2 0.5 copy-start.4
  223.8 18.2 %copy-start.7 = (f32[2560]{0:T(1024)S(1)}, f32[2560]{0:T(1024)}, u32[]{:S(2)}) copy-start(f32[2560]{0:T(1024)} %param.17) | copy-start | bytes 30724
  240.0 2.9 %collective-permute-start.2 = (f32[2,768,1]{1,0,2:T(2,128)S(1)}, f32[2,768,1]{1,0,2:T(2,128)S(1)}, u32[]{:S(2)}, u32[]{:S(2)}) collective-permute-start(f32[2,768,1]{1,0,2:T(2,128)S(1)} %copy.12), channel_id=1, source_target_pairs={{0,1},{1,0},{2,3},{3,2},{4,5},{5,4},{6,7},{7,6},{8,9},{9,8},{10,11... | collective-permute-start | bytes 18440 | tf_op jit(solution)/shard_map/ppermute | solution.py:497
  248.8 4.1 %collective-permute-start.3 = (bf16[768,1280]{1,0:T(8,128)(2,1)S(1)}, bf16[768,1280]{1,0:T(8,128)(2,1)S(1)}, u32[]{:S(2)}, u32[]{:S(2)}) collective-permute-start(bf16[768,1280]{1,0:T(8,128)(2,1)S(1)} %get-tuple-element.22), channel_id=1, source_target_pairs={{0,1},{1,0},{2,3},{3,2},{4,5},{5,4},{6,7},{7,6},{8,9},{9,8},{10,11... | collective-permute-start | bytes 5898248 | tf_op jit(solution)/shard_map/ppermute | solution.py:500

commit v2 on v0

v2 whole, which is shorter than its diff:
```python
import jax
import jax.numpy as jnp
import numpy as np
from jax import lax
from jax.experimental import pallas as pl
from jax.experimental.pallas import tpu as pltpu
from jax.sharding import Mesh
from jax.sharding import PartitionSpec as P

BLOCK = 256
CHUNK = 128
HALO = 16
LANES = 128
COUNT = 64
OWNERS = 32
LOG2E = 1.4426950408889634
AXES = ("y", "z", "xh", "xl")
F32 = jnp.float32
BF16 = jnp.bfloat16
MESH = pl.DeviceIdType.MESH
ORDERS = (("x", "y", "z"), ("y", "z", "x"), ("z", "x", "y"))
SLOTS = ((0, 0, 1), (0, 1, 1), (-1, 0, 1), (0, 1, -1), (0, 0, -1), (1, 1, -1))


def split3(value):
    hi = value.astype(BF16)
    rest = value - hi.astype(F32)
    mid = rest.astype(BF16)
    lo = (rest - mid.astype(F32)).astype(BF16)
    return hi, mid, lo


def split2(value):
    hi = value.astype(BF16)
    lo = (value - hi.astype(F32)).astype(BF16)
    return hi, lo


def dot(a, b):
    return jnp.dot(a, b, preferred_element_type=F32)


def layer_kernel(
    live_ref, edge_ref, tokens_ref, pieces_ref, params_ref, heads_ref, spread_ref, tri_ref,
    out_ref,
    rows_in, weight, proj, far_map, y_all, map_all, cum_all, state, total, parts, block, arrived,
    starts, decays, factors, incoming, square, far_square, staged, live,
    part_send, part_recv, token_sem, token_send, token_recv, edge_send, edge_recv, live_send,
    live_recv, gather_send, gather_recv, map_send, map_recv, piece_send, piece_recv, decay_send,
    decay_recv, back_send, back_recv, square_send, square_recv, out_send, out_recv,
):
    y, z, xh, xl = (lax.axis_index(axis) for axis in AXES)
    core = lax.axis_index("core")
    x = xh * 2 + xl
    here = {"y": y, "z": z, "x": x}
    me = (y * 4 + z) * 4 + x
    slots, model = tokens_ref.shape
    inner = model // 2
    wide = inner // 2
    group_width = weight.shape[-1]
    partner = {"core": 1 - core}
    core_lane = pl.multiple_of(core * inner, LANES)

    def device(index):
        return {
            "y": index // 16,
            "z": lax.rem(index // 4, 4),
            "xh": lax.rem(index // 2, 2),
            "xl": lax.rem(index, 2),
        }

    def remote(source, target, send, recv, where):
        return pltpu.make_async_remote_copy(
            src_ref=source, dst_ref=target, send_sem=send, recv_sem=recv,
            device_id=where, device_id_type=MESH,
        )

    barrier = pltpu.get_barrier_semaphore()

    @pl.loop(1, 2 * COUNT)
    def _(i):
        other = lax.rem(me * 2 + core + i, 2 * COUNT)
        pl.semaphore_signal(
            barrier, inc=1, device_id={**device(other // 2), "core": lax.rem(other, 2)},
            device_id_type=MESH,
        )

    pl.semaphore_wait(barrier, 2 * COUNT - 1)

    my_part = xl * 2 + core

    def part_copy(step):
        target = lax.rem(my_part + step, 4)
        return remote(
            pieces_ref.at[target], parts.at[my_part], part_send.at[step], part_recv.at[step],
            {"xl": target // 2, "core": lax.rem(target, 2)},
        )

    def part_arrival(step):
        source = lax.rem(my_part + 4 - step, 4)
        return remote(
            pieces_ref.at[0], parts.at[source], part_send.at[step], part_recv.at[step], partner
        )

    for step in (1, 2, 3):
        part_copy(step).start()
    parts[my_part] = pieces_ref[my_part]

    own_rows = pltpu.make_async_copy(tokens_ref, rows_in.at[core, pl.ds(HALO, slots)], token_sem)
    own_rows.start()
    rows_copy = remote(
        tokens_ref, rows_in.at[core, pl.ds(HALO, slots)], token_send, token_recv, partner
    )
    live[core] = live_ref[...]
    live_copy = remote(live_ref, live.at[core], live_send, live_recv, partner)
    live_copy.start()

    def edge_copy(side):
        return remote(
            edge_ref, rows_in.at[core, pl.ds(0, HALO)], edge_send.at[side], edge_recv.at[core],
            {**device(me + 1), "core": side},
        )

    @pl.when(me < COUNT - 1)
    def _():
        for side in range(2):
            edge_copy(side).start()

    @pl.when(me == 0)
    def _():
        rows_in[:, 0:HALO, :] = jnp.zeros((2, HALO, model), BF16)

    for step in (1, 2, 3):
        part_arrival(step).wait_recv()
    block[...] = jnp.concatenate([parts[i].astype(F32) for i in range(4)], axis=0).astype(BF16)

    near = lambda axis, step: lax.rem(here[axis] + step + 4, 4)
    unit = group_width // 6

    def along(axis, step):
        coordinate = near(axis, step)
        if axis == "x":
            return {"xh": coordinate // 2, "xl": lax.rem(coordinate, 2)}
        return {axis: coordinate}

    def region(group, color, half, spot):
        wy, wz, wx = (spot[axis] for axis in ("y", "z", "x"))
        low, high = (slice(None), slice(None)) if wx is None else (lax.rem(wx, 2), wx // 2)
        wy = slice(None) if wy is None else wy
        wz = slice(None) if wz is None else wz
        return weight.at[group, low, wy, wz, high, :, pl.ds((color * 2 + half) * unit, unit)]

    def spot_of(color, stage, coordinate):
        spot = dict(here)
        for axis in ORDERS[color][:stage]:
            spot[axis] = None
        spot[ORDERS[color][stage]] = coordinate
        return spot

    def ring_copy(group, color, stage, slot):
        offset, half, step = SLOTS[slot]
        axis = ORDERS[color][stage]
        target = region(group, color, half, spot_of(color, stage, near(axis, offset)))
        source = target
        if stage == 0 and offset == 0:
            source = block.at[:, pl.ds(group * group_width + (color * 2 + half) * unit, unit)]
        return remote(
            source, target, gather_send.at[group, color, stage, slot],
            gather_recv.at[group, color, stage, slot], along(axis, step),
        )

    def ring_arrival(group, color, stage, slot):
        offset, half, step = SLOTS[slot]
        axis = ORDERS[color][stage]
        target = region(group, color, half, spot_of(color, stage, near(axis, offset - step)))
        return remote(
            target, target, gather_send.at[group, color, stage, slot],
            gather_recv.at[group, color, stage, slot], along(axis, step),
        )

    def ring_start(group, stage):
        for color in range(3):
            if stage:
                for slot in (1, 2, 4, 5):
                    ring_arrival(group, color, stage - 1, slot).wait_recv()
            for slot in (0, 3, 1, 4):
                ring_copy(group, color, stage, slot).start()

    def ring_forward(group, stage):
        for color in range(3):
            ring_arrival(group, color, stage, 0).wait_recv()
            ring_copy(group, color, stage, 2).start()
            ring_arrival(group, color, stage, 3).wait_recv()
            ring_copy(group, color, stage, 5).start()

    def ring_finish(group):
        for color in range(3):
            for slot in (1, 2, 4, 5):
                ring_arrival(group, color, 2, slot).wait_recv()

    ring_start(0, 0)
    rows_copy.start()
    for group in range(2):
        weight[group, xl, y, z, xh] = block[:, group * group_width : (group + 1) * group_width]
    ring_forward(0, 0)
    ring_start(0, 1)
    ring_start(1, 0)
    ring_forward(0, 1)
    ring_forward(1, 0)
    ring_start(0, 2)
    ring_forward(0, 2)
    ring_start(1, 1)
    own_rows.wait()
    rows_copy.wait_send()
    remote(
        tokens_ref, rows_in.at[1 - core, pl.ds(HALO, slots)], token_send, token_recv, partner
    ).wait_recv()
    remote(live_ref, live.at[1 - core], live_send, live_recv, partner).wait_recv()

    @pl.when(me > 0)
    def _():
        for side in range(2):
            remote(
                edge_ref, rows_in.at[side, pl.ds(0, HALO)], edge_send.at[side], edge_recv.at[side],
                partner,
            ).wait_recv()

    ring_finish(0)

    def project(group, first, last):
        @pl.loop(first, last)
        def _(i):
            seq = lax.rem(i, 2)
            tile = i // 2
            columns = pl.ds(pl.multiple_of(lax.rem(tile, 3) * 2 * LANES, LANES), 2 * LANES)
            matrix = weight[group, tile // 3, :, :, :, :, columns].reshape(model, 2 * LANES)
            proj[seq, :, pl.ds(pl.multiple_of(tile * 2 * LANES, LANES), 2 * LANES)] = dot(
                rows_in[seq], matrix
            ).astype(BF16)

    map_copy = remote(proj.at[:, :, pl.ds(0, LANES)], far_map, map_send, map_recv, partner)
    project(0, 0, 4)
    map_copy.start()
    ring_forward(1, 1)
    project(0, 4, 8)
    ring_start(1, 2)
    project(0, 8, 12)
    map_copy.wait()

    def slice_of(ref, seq, k):
        row = pl.multiple_of(k // 2 * 8, 8)
        column = pl.multiple_of(lax.rem(k, 2) * wide, LANES)
        return ref.at[seq, pl.ds(row, 8), pl.ds(column, wide)]

    my_k = (y * 4 + z) * 2 + xh
    my_seq = lax.rem(y + z + xl, 2)

    def owner(seq, k):
        oy, oz = k // 8, lax.rem(k // 2, 4)
        return {"y": oy, "z": oz, "xh": lax.rem(k, 2), "xl": lax.rem(seq + oy + oz, 2)}

    def piece(seq, k, slot):
        return remote(
            slice_of(state, seq, k), arrived.at[slot], piece_send.at[seq * OWNERS + k],
            piece_recv.at[slot], owner(seq, k),
        )

    def decay_copy(seq, k, slot):
        return remote(
            total.at[seq], decays.at[slot], decay_send.at[seq * OWNERS + k],
            decay_recv.at[slot], owner(seq, k),
        )

    def back(index, seq, k):
        return remote(
            starts.at[index], slice_of(incoming, seq, k), back_send.at[index],
            back_recv.at[seq * OWNERS + k], device(index),
        )

    rows = lax.broadcasted_iota(jnp.int32, (CHUNK, LANES), 0)
    columns = lax.broadcasted_iota(jnp.int32, (CHUNK, LANES), 1)

    def wide_row(index):
        return jnp.concatenate(
            [params_ref[index : index + 1, pl.ds(core_lane, inner)], params_ref[index : index + 1, model:]],
            axis=1,
        )

    def scan_chunk(seq, chunk):
        row0 = pl.multiple_of(chunk * CHUNK, CHUNK)
        window = pl.ds(row0, CHUNK + HALO)
        near_map = proj[seq, window, 0:LANES].astype(F32)
        other_map = far_map[seq, window, :].astype(F32)
        mixed = jnp.concatenate(
            [
                proj[seq, window, 2 * LANES :].astype(F32),
                jnp.where(core == 0, near_map, other_map),
                jnp.where(core == 0, other_map, near_map),
            ],
            axis=1,
        )
        conv = wide_row(4)
        for k in range(4):
            conv = conv + wide_row(k) * mixed[HALO - 3 + k : HALO - 3 + k + CHUNK]
        act = (conv * jax.nn.sigmoid(conv)).astype(BF16)
        value = act[:, :inner]
        in_map = act[:, inner : inner + LANES]
        out_map = act[:, inner + LANES :]

        raw = proj[seq, pl.ds(row0 + HALO, CHUNK), LANES : 2 * LANES].astype(F32)
        raw = raw + heads_ref[core, 0:1, :]
        tail = jnp.exp(-jnp.abs(raw))
        series = tail * (1.0 - tail * (0.5 - tail * (1.0 / 3.0 - 0.25 * tail)))
        step = jnp.maximum(raw, 0.0) + jnp.where(tail < 0.01, series, jnp.log(1.0 + tail))
        step = jnp.where((rows + row0).astype(F32) < live[seq, 0:1, :], step, 0.0)
        log_decay = -(step * heads_ref[core, 1:2, :]) * LOG2E
        cum = dot(tri_ref[...], jnp.concatenate(split3(log_decay), axis=0))
        shifted = jnp.where(step > 0.0, cum - jnp.log(step) * LOG2E, 1e30).T
        causal = rows >= columns
        scores = lax.dot_general(
            out_map, in_map, (((1,), (1,)), ((), ())), preferred_element_type=F32
        )
        before = state[seq]
        growth = dot(jnp.concatenate(split3(jnp.exp2(cum)), axis=1), spread_ref[...])
        reach = dot(
            jnp.concatenate([out_map, out_map], axis=1), jnp.concatenate(split2(before), axis=0)
        )
        base = growth * reach + params_ref[6:7, pl.ds(core_lane, inner)] * value.astype(F32)
        left = columns < LANES // 2
        zero = jnp.zeros((CHUNK, LANES), BF16)
        for tile in range(inner // LANES):
            lanes = slice(tile * LANES, (tile + 1) * LANES)
            result = base[:, lanes]
            for side in range(2):
                head = tile * 2 + side
                reached = jnp.where(
                    causal, cum[:, head : head + 1] - shifted[head : head + 1, :], -1e30
                )
                mixing = jnp.exp2(reached) * scores
                kept = jnp.where(left if side == 0 else ~left, value[:, lanes], zero)
                result = result + dot(
                    jnp.concatenate(split2(mixing), axis=1), jnp.concatenate([kept, kept], axis=0)
                )
            y_all[seq, pl.ds(row0, CHUNK), lanes] = result

        last = cum[CHUNK - 1 : CHUNK, :]
        to_end = jnp.exp2(last - cum) * step
        weighted = value.astype(F32) * dot(
            jnp.concatenate(split3(to_end), axis=1), spread_ref[...]
        )
        added = lax.dot_general(
            jnp.concatenate([in_map, in_map], axis=0),
            jnp.concatenate(split2(weighted), axis=0),
            (((0,), (0,)), ((), ())),
            preferred_element_type=F32,
        )
        state[seq] = growth[CHUNK - 1 : CHUNK, :] * before + added
        map_all[seq, pl.ds(row0, CHUNK), :] = out_map
        cum_all[seq, pl.ds(row0, CHUNK), :] = cum + total[seq]
        total[seq] = total[seq] + last

    state[...] = jnp.zeros_like(state)
    total[...] = jnp.zeros_like(total)
    ring_forward(1, 2)

    @pl.loop(0, 2)
    def _(seq):
        @pl.loop(0, slots // CHUNK)
        def _(chunk):
            scan_chunk(seq, chunk)

        @pl.loop(0, OWNERS)
        def _(i):
            k = lax.rem(my_k + i, OWNERS)
            mine = jnp.logical_and(i == 0, seq == my_seq)

            @pl.when(jnp.logical_not(mine))
            def _():
                decay_copy(seq, k, me).start()
                piece(seq, k, me).start()

            @pl.when(mine)
            def _():
                arrived[me] = slice_of(state, seq, k)[...]
                decays[me] = total[seq]

    def compose_all():
        @pl.loop(1, COUNT)
        def _(i):
            peer = lax.rem(me + i, COUNT)
            decay_copy(my_seq, my_k, peer).wait_recv()
            piece(my_seq, my_k, peer).wait_recv()

        column = pl.multiple_of(lax.rem(my_k, 2) * wide, LANES)
        decay = jnp.exp2(decays[...].reshape(COUNT, LANES))
        factors[...] = dot(
            jnp.concatenate(split3(decay), axis=1), spread_ref[:, pl.ds(column, wide)]
        )

        def compose(index, carry):
            starts[index] = carry
            return factors[pl.ds(index, 1), :] * carry + arrived[index]

        lax.fori_loop(0, COUNT, compose, jnp.zeros((8, wide), F32))

        @pl.loop(1, COUNT)
        def _(i):
            back(lax.rem(me + i, COUNT), my_seq, my_k).start()

        slice_of(incoming, my_seq, my_k)[...] = starts[me]

    pl.when(my_seq == 0)(compose_all)
    ring_finish(1)
    project(1, 0, 4)
    pl.when(my_seq == 1)(compose_all)
    project(1, 4, 10)

    def square_copy(seq):
        return remote(
            square.at[seq], far_square.at[seq], square_send.at[seq], square_recv.at[seq], partner
        )

    def gate_sequence(seq):
        @pl.loop(0, OWNERS)
        def _(k):
            @pl.when(jnp.logical_not(jnp.logical_and(k == my_k, my_seq == seq)))
            def _():
                back(me, seq, k).wait_recv()

        start = jnp.concatenate(split2(incoming[seq]), axis=0)

        @pl.loop(0, slots // CHUNK)
        def _(chunk):
            row0 = pl.multiple_of(chunk * CHUNK, CHUNK)
            here_rows = pl.ds(row0, CHUNK)
            growth = dot(
                jnp.concatenate(split3(jnp.exp2(cum_all[seq, here_rows, :])), axis=1),
                spread_ref[...],
            )
            out_map = map_all[seq, here_rows, :]
            reach = dot(jnp.concatenate([out_map, out_map], axis=1), start)
            gate = proj[seq, pl.ds(row0 + HALO, CHUNK), 0:inner].astype(F32)
            gated = (y_all[seq, here_rows, :] + growth * reach) * (gate * jax.nn.sigmoid(gate))
            y_all[seq, here_rows, :] = gated
            square[seq, here_rows, :] = jnp.broadcast_to(
                jnp.sum(gated * gated, axis=1, keepdims=True), (CHUNK, LANES)
            )

        square_copy(seq).start()

    for seq in range(2):
        gate_sequence(seq)

    out_copy = remote(staged, out_ref.at[:, pl.ds(core_lane, inner)], out_send, out_recv, partner)
    for seq in range(2):
        square_copy(seq).wait_recv()

        def normed(row0):
            here_rows = pl.ds(row0, CHUNK)
            mean = (square[seq, here_rows, 0:1] + far_square[seq, here_rows, 0:1]) / model
            result = (
                y_all[seq, here_rows, :]
                * lax.rsqrt(mean + 1e-05)
                * params_ref[5:6, pl.ds(core_lane, inner)]
            )
            kept = (rows[:, 0:1] + row0).astype(F32) < live[seq, 0:1, 0:1]
            return jnp.where(kept, result, 0.0).astype(BF16)

        @pl.when(core == seq)
        def _():
            @pl.loop(0, slots // CHUNK)
            def _(chunk):
                row0 = pl.multiple_of(chunk * CHUNK, CHUNK)
                out_ref[pl.ds(row0, CHUNK), pl.ds(core_lane, inner)] = normed(row0)

        @pl.when(core != seq)
        def _():
            @pl.loop(0, slots // CHUNK)
            def _(chunk):
                row0 = pl.multiple_of(chunk * CHUNK, CHUNK)
                staged[pl.ds(row0, CHUNK), :] = normed(row0)

            out_copy.start()

    for step in (1, 2, 3):
        part_copy(step).wait_send()
    live_copy.wait_send()

    @pl.when(me < COUNT - 1)
    def _():
        for side in range(2):
            edge_copy(side).wait_send()

    for group in range(2):
        for stage in range(3):
            for color in range(3):
                for slot in range(6):
                    ring_copy(group, color, stage, slot).wait_send()

    @pl.loop(0, 2 * OWNERS)
    def _(i):
        seq = i // OWNERS
        k = lax.rem(i, OWNERS)

        @pl.when(jnp.logical_not(jnp.logical_and(k == my_k, my_seq == seq)))
        def _():
            piece(seq, k, me).wait_send()
            decay_copy(seq, k, me).wait_send()

    @pl.loop(1, COUNT)
    def _(i):
        back(lax.rem(me + i, COUNT), my_seq, my_k).wait_send()

    for seq in range(2):
        square_copy(seq).wait_send()
    out_copy.wait_send()
    far_lane = pl.multiple_of((1 - core) * inner, LANES)
    remote(
        staged, out_ref.at[:, pl.ds(far_lane, inner)], out_send, out_recv, partner
    ).wait_recv()


def layer_call(live, edge, tokens, pieces, params, heads, spread, tri):
    slots, model = tokens.shape
    inner = model // 2
    columns = pieces.shape[2]
    padded = slots + HALO
    vmem = pl.BlockSpec(memory_space=pltpu.VMEM)
    dma = pltpu.SemaphoreType.DMA
    return pl.pallas_call(
        layer_kernel,
        out_shape=jax.ShapeDtypeStruct((slots, model), BF16),
        in_specs=[vmem, vmem, pl.BlockSpec(memory_space=pl.ANY)] + [vmem] * 5,
        out_specs=vmem,
        scratch_shapes=[
            pltpu.VMEM((2, padded, model), BF16),
            pltpu.VMEM((2, 2, 4, 4, 2, model // 32, columns // 2), BF16),
            pltpu.VMEM((2, padded, columns), BF16),
            pltpu.VMEM((2, padded, LANES), BF16),
            pltpu.VMEM((2, slots, inner), F32),
            pltpu.VMEM((2, slots, LANES), BF16),
            pltpu.VMEM((2, slots, LANES), F32),
            pltpu.VMEM((2, LANES, inner), F32),
            pltpu.VMEM((2, 1, LANES), F32),
            pltpu.VMEM(pieces.shape, BF16),
            pltpu.VMEM((model // 32, columns), BF16),
            pltpu.VMEM((COUNT, 8, inner // 2), F32),
            pltpu.VMEM((COUNT, 8, inner // 2), F32),
            pltpu.VMEM((COUNT, 1, LANES), F32),
            pltpu.VMEM((COUNT, inner // 2), F32),
            pltpu.VMEM((2, LANES, inner), F32),
            pltpu.VMEM((2, slots, LANES), F32),
            pltpu.VMEM((2, slots, LANES), F32),
            pltpu.VMEM((slots, inner), BF16),
            pltpu.VMEM((2, 8, LANES), F32),
            dma((4,)), dma((4,)),
            dma, dma, dma,
            dma((2,)), dma((2,)),
            dma, dma,
            dma((2, 3, 3, 6)), dma((2, 3, 3, 6)),
            dma, dma,
            dma((COUNT,)), dma((COUNT,)), dma((COUNT,)), dma((COUNT,)),
            dma((COUNT,)), dma((COUNT,)),
            dma((2,)), dma((2,)),
            dma, dma,
        ],
        compiler_params=pltpu.CompilerParams(
            collective_id=0, has_side_effects=True, vmem_limit_bytes=67043328
        ),
        name="layer",
    )(live, edge, tokens, pieces, params, heads, spread, tri)


def local(
    tokens, bounds, in_weight, conv_weight, conv_bias, dt_bias, decay_rate, skip_gain, norm_gain
):
    slots, model = tokens.shape[1:]
    width = norm_gain.shape[0]
    inner = width // 2
    heads = decay_rate.shape[0] // 2
    rows = in_weight.shape[0]

    low, high = 4 * LANES, 6 * LANES
    pieces = []
    for side in range(2):
        for core in range(2):
            value = width + core * inner
            gate = core * inner
            if side == 0:
                raw = 2 * width + 2 * LANES + core * heads
                pieces += [
                    in_weight[:, 2 * width + core * LANES : 2 * width + (core + 1) * LANES],
                    jnp.pad(in_weight[:, raw : raw + heads], ((0, 0), (0, LANES - heads))),
                    in_weight[:, value : value + low],
                    in_weight[:, gate : gate + high],
                ]
            else:
                pieces += [
                    in_weight[:, value + low : value + inner],
                    in_weight[:, gate + high : gate + inner],
                    jnp.zeros((rows, 2 * high - inner), BF16),
                ]
    pieces = jnp.concatenate(pieces, axis=1).reshape(rows, 4, 2 * high).swapaxes(0, 1)

    blocks = bounds[0, 0, 1] - bounds[0, 0, 0]
    edge = lax.dynamic_slice_in_dim(tokens[0], blocks * BLOCK - HALO, HALO, 0)
    live = jnp.full((8, LANES), (blocks * BLOCK).astype(F32))
    stretch = lambda a: jnp.pad(a, (0, conv_bias.shape[0] - width))[None]
    params = jnp.concatenate(
        [
            conv_weight, conv_bias[None], stretch(norm_gain),
            stretch(jnp.repeat(skip_gain, width // (2 * heads))),
            jnp.zeros((1, conv_bias.shape[0]), F32),
        ]
    )
    per_head = jnp.stack([dt_bias.reshape(2, heads), decay_rate.reshape(2, heads)], axis=1)
    per_head = jnp.pad(per_head, ((0, 0), (0, 6), (0, LANES - heads)))
    spread = (np.arange(inner)[None, :] // (inner // heads) == np.arange(LANES)[:, None])
    spread = jnp.asarray(np.concatenate([spread] * 3, axis=0), BF16)
    tri = jnp.asarray(np.concatenate([np.tril(np.ones((CHUNK, CHUNK)))] * 3, axis=1), BF16)
    out = layer_call(live, edge, tokens[0], pieces, params, per_head, spread, tri)
    return out[None]


def solution(mesh):
    split = Mesh(mesh.devices.reshape(4, 4, 2, 2, 2), AXES + ("core",))
    return jax.shard_map(
        local,
        mesh=split,
        in_specs=(
            P("core", AXES, None),
            P("core", AXES, None),
            P(AXES + ("core",), None),
            P(), P(), P(), P(), P(), P(),
        ),
        out_specs=P("core", AXES, None),
        check_vma=False,
    )
```

time: 460 us -> 186 us (0.40); the launches traced: 452 us -> 185 us
  waiting for transfers between devices: 251 us -> 0 us
  Pallas kernels: 0 us -> 161 us
  matrix products: 57 us -> 0 us
  other arithmetic: 46.4 us -> 0.6 us
  local copies, waits for them, and re-layouts: 54 us -> 22.2 us
  blocking collectives: 24.1 us -> 0 us
  between operations: 15.9 us -> 1.34 us
    all_gather x4 -> x0, waiting for transfers between devices: 251 us -> none  [the longest x3 141 us: prefix_by_axis(): pieces = jax.tree.map(lambda part: lax.all_gather(part, axis), total)]
    pallas_call x0 -> x1, Pallas kernels: none -> 161 us  [layer_call(): pl.pallas_call(layer_kernel, out_shape=jax.ShapeDtypeStruct((slots, model...]
    dot_general x13 -> x0, matrix products: 57 us -> none  [the longest x1 29 us: local(): jnp.dot(own_rows, lax.all_gather(in_weight, SEQ_FSDP, axis=0, tiled=True)...]
    unnamed x60 -> x14, local copies, waits for them, and re-layouts: 41 us -> 11.8 us
    all_gather x2 -> x0, blocking collectives: 16.3 us -> none  [prefix_by_axis(): pieces = jax.tree.map(lambda part: lax.all_gather(part, axis), total)]
    convert_element_type x1 -> x0, other arithmetic: 16 us -> none  [local(): conv_out = jax.nn.silu(convolved).astype(jnp.bfloat16)]
    add x3 -> x0, other arithmetic: 16 us -> none  [compose(): later[0][:, None, None] * earlier[1] + later[1]]
    unnamed x1 -> x0, blocking collectives: 7.71 us -> none
  transfers between devices with their start and end apart: 5 -> 0, of which waited for: 4 -> 0; matrix products, arithmetic and copies ran while one was open for 3% -> 0% of each run, Pallas kernels for 0% -> 0%
where the time goes in v2:
time: 186 us; the launch traced here: 185 us
  Pallas kernels  161 us (87%)
  local copies, waits for them, and re-layouts  22.2 us (12%)
    pallas_call x1, Pallas kernels, layer_call(): pl.pallas_call(layer_kernel, out_shape=jax.ShapeDtypeStruct((slots, model...  161 us
    unnamed x14, local copies, waits for them, and re-layouts  11.8 us

profile of v2, /device:TPU:1, one launch (start us, length us, event | category | flops | bytes accessed | tf_op | source)
XLA Modules:
  0.0 185.2 jit_solution(12571432564255867668)
XLA Ops:
  0.0 0.7 stack_reshape.6
  0.7 0.7 stack_reshape.7
  1.5 1.3 fusion.1
  4.1 0.6 broadcast_in_dim.21.live_ref
  4.7 0.6 select_maximum_fusion.heads_ref
  5.3 0.7 broadcast_in_dim.22
  6.0 0.7 pad.20
  6.7 0.8 fusion
  7.6 0.7 broadcast_in_dim.24
  8.3 0.1 reshape.16
  8.4 1.5 concatenate.7.params_ref
  9.9 1.5 dynamic-slice_bitcast_fusion.edge_ref
  11.4 0.7 constant_dynamic-update-slice_fusion.9
  12.1 0.7 constant_dynamic-update-slice_fusion.7
  12.9 0.8 slice_dynamic-update-slice_fusion.3
  13.7 0.7 constant_dynamic-update-slice_fusion.6
  14.4 0.7 constant_dynamic-update-slice_fusion.4
  15.1 0.8 slice_dynamic-update-slice_fusion.2
  15.9 0.8 slice_dynamic-update-slice_fusion.1
  16.6 0.7 constant_dynamic-update-slice_fusion.3
  17.4 0.8 slice_dynamic-update-slice_fusion
  18.2 0.7 constant_dynamic-update-slice_fusion.1
  18.9 0.1 reshape.15
  19.0 0.8 copy.18
  19.8 161.1 %layer.1 = bf16[768,2560]{1,0:T(8,128)(2,1)} custom-call(f32[8,128]{1,0:T(8,128)} %broadcast_in_dim.21.live_ref, bf16[16,2560]{1,0:T(8,128)(2,1)} %dynamic-slice_bitcast_fusion.edge_ref, bf16[768,2560]{1,0:T(8,128)(2,1)} %bitcast.13, bf16[4,20,1536]{2,1,0:T(8,128)(2,1)} %bitcast.14, f32[8,2816]{1,0:T(8,128)} %concatenate.7.params_ref, ...), custom_call_target="tpu_custom_call" | custom-call | tf_op jit(solution)/shard_map/layer/pallas_call | solution.py:530
  180.9 4.3 %copy.33 = bf16[1,768,2560]{2,1,0:T(8,128)(2,1)} copy(bf16[1,768,2560]{2,1,0:T(8,128)(2,1)} %bitcast.12) | data formatting | bytes 7864320
  (8 shorter events, 0.1 us)

commit v3 on v2

--- a/solution.py
+++ b/solution.py
@@ -1,6 +1,5 @@
 import jax
 import jax.numpy as jnp
-import numpy as np
 from jax import lax
 from jax.experimental import pallas as pl
 from jax.experimental.pallas import tpu as pltpu
@@ -19,6 +18,11 @@
 BF16 = jnp.bfloat16
 MESH = pl.DeviceIdType.MESH
 ORDERS = (("x", "y", "z"), ("y", "z", "x"), ("z", "x", "y"))
+GROUPS = (
+    (((0, 128), (128, 128), (256, 128)), 48),
+    (((384, 128), (512, 128), (640, 128)), 32),
+    (((768, 256), (1024, 256), (1280, 128)), 48),
+)
 SLOTS = ((0, 0, 1), (0, 1, 1), (-1, 0, 1), (0, 1, -1), (0, 0, -1), (1, 1, -1))
 
 
@@ -41,11 +45,12 @@
 
 
 def layer_kernel(
-    live_ref, edge_ref, tokens_ref, pieces_ref, params_ref, heads_ref, spread_ref, tri_ref,
+    bounds_ref, tokens_ref, shard_ref, taps_ref, bias_ref, dt_ref, decay_ref, skip_ref, gain_ref,
     out_ref,
-    rows_in, weight, proj, far_map, y_all, map_all, cum_all, state, total, parts, block, arrived,
+    rows_in, weight, act_all, raw_all, spread_ref, tri_ref, heads, skips, pieces, ends, edge,
+    far_map, y_all, map_all, cum_all, state, total, parts, block, arrived,
     starts, decays, factors, incoming, square, far_square, staged, live,
-    part_send, part_recv, token_sem, token_send, token_recv, edge_send, edge_recv, live_send,
+    end_sem, part_send, part_recv, token_sem, token_send, token_recv, edge_send, edge_recv, live_send,
     live_recv, gather_send, gather_recv, map_send, map_recv, piece_send, piece_recv, decay_send,
     decay_recv, back_send, back_recv, square_send, square_recv, out_send, out_recv,
 ):
@@ -54,10 +59,11 @@
     x = xh * 2 + xl
     here = {"y": y, "z": z, "x": x}
     me = (y * 4 + z) * 4 + x
-    slots, model = tokens_ref.shape
+    slots, model = tokens_ref.shape[1:]
     inner = model // 2
     wide = inner // 2
-    group_width = weight.shape[-1]
+    head_count = dt_ref.shape[1] // 2
+    shard = tokens_ref.at[0]
     partner = {"core": 1 - core}
     core_lane = pl.multiple_of(core * inner, LANES)
 
@@ -85,6 +91,45 @@
             device_id_type=MESH,
         )
 
+    own_rows = pltpu.make_async_copy(shard, rows_in.at[core, pl.ds(HALO, slots)], token_sem)
+    own_rows.start()
+    end_copies = [
+        pltpu.make_async_copy(
+            shard.at[pl.ds((i + 1) * BLOCK - HALO, HALO)], ends.at[i], end_sem.at[i]
+        )
+        for i in range(slots // BLOCK)
+    ]
+    for copy in end_copies:
+        copy.start()
+
+    t = LANES
+    for side in range(2):
+        for other in range(2):
+            index = side * 2 + other
+            value, gate = model + other * inner, other * inner
+            if side == 0:
+                maps = 2 * model + other * t
+                raw = 2 * model + 2 * t
+                pieces[index, :, 0:t] = shard_ref[:, maps : maps + t]
+                pieces[index, :, t : 2 * t] = jnp.zeros((shard_ref.shape[0], t), BF16)
+                pieces[index, :, t : t + 2 * head_count] = shard_ref[:, raw : raw + 2 * head_count]
+                pieces[index, :, 2 * t : 3 * t] = shard_ref[:, value : value + t]
+                pieces[index, :, 3 * t : 6 * t] = shard_ref[:, value + 4 * t : value + 7 * t]
+                pieces[index, :, 6 * t :] = shard_ref[:, gate : gate + 5 * t]
+            else:
+                pieces[index, :, 0 : 3 * t] = shard_ref[:, value + t : value + 4 * t]
+                pieces[index, :, 3 * t : 6 * t] = shard_ref[:, value + 7 * t : value + 10 * t]
+                pieces[index, :, 6 * t :] = shard_ref[:, gate + 5 * t : gate + 10 * t]
+
+    block_count = bounds_ref[0, 0, 1] - bounds_ref[0, 0, 0]
+    live[core] = jnp.full((8, LANES), (block_count * BLOCK).astype(F32))
+    heads[...] = jnp.zeros_like(heads)
+    for i, ref in enumerate((dt_ref, decay_ref, skip_ref)):
+        heads[i : i + 1, 0 : 2 * head_count] = ref[...]
+    both = heads[...]
+    mine = jnp.where(core == 0, both, pltpu.roll(both, LANES - head_count, 1))
+    lane8 = lax.broadcasted_iota(jnp.int32, (8, LANES), 1)
+    heads[...] = jnp.where(lane8 < head_count, mine, 0.0)
     pl.semaphore_wait(barrier, 2 * COUNT - 1)
 
     my_part = xl * 2 + core
@@ -92,32 +137,35 @@
     def part_copy(step):
         target = lax.rem(my_part + step, 4)
         return remote(
-            pieces_ref.at[target], parts.at[my_part], part_send.at[step], part_recv.at[step],
+            pieces.at[target], parts.at[my_part], part_send.at[step], part_recv.at[step],
             {"xl": target // 2, "core": lax.rem(target, 2)},
         )
 
     def part_arrival(step):
         source = lax.rem(my_part + 4 - step, 4)
         return remote(
-            pieces_ref.at[0], parts.at[source], part_send.at[step], part_recv.at[step], partner
+            pieces.at[0], parts.at[source], part_send.at[step], part_recv.at[step], partner
         )
 
     for step in (1, 2, 3):
         part_copy(step).start()
-    parts[my_part] = pieces_ref[my_part]
-
-    own_rows = pltpu.make_async_copy(tokens_ref, rows_in.at[core, pl.ds(HALO, slots)], token_sem)
-    own_rows.start()
+    parts[my_part] = pieces[my_part]
+
     rows_copy = remote(
-        tokens_ref, rows_in.at[core, pl.ds(HALO, slots)], token_send, token_recv, partner
+        shard, rows_in.at[core, pl.ds(HALO, slots)], token_send, token_recv, partner
     )
-    live[core] = live_ref[...]
-    live_copy = remote(live_ref, live.at[core], live_send, live_recv, partner)
+    live_copy = remote(live.at[core], live.at[core], live_send, live_recv, partner)
     live_copy.start()
+    for copy in end_copies:
+        copy.wait()
+    chosen = ends[0].astype(F32)
+    for i in range(1, slots // BLOCK):
+        chosen = jnp.where(block_count == i + 1, ends[i].astype(F32), chosen)
+    edge[...] = chosen.astype(BF16)
 
     def edge_copy(side):
         return remote(
-            edge_ref, rows_in.at[core, pl.ds(0, HALO)], edge_send.at[side], edge_recv.at[core],
+            edge, rows_in.at[core, pl.ds(0, HALO)], edge_send.at[side], edge_recv.at[core],
             {**device(me + 1), "core": side},
         )
 
@@ -135,7 +183,6 @@
     block[...] = jnp.concatenate([parts[i].astype(F32) for i in range(4)], axis=0).astype(BF16)
 
     near = lambda axis, step: lax.rem(here[axis] + step + 4, 4)
-    unit = group_width // 6
 
     def along(axis, step):
         coordinate = near(axis, step)
@@ -143,12 +190,18 @@
             return {"xh": coordinate // 2, "xl": lax.rem(coordinate, 2)}
         return {axis: coordinate}
 
+    def part_of(group, color, half):
+        start, size = GROUPS[group][0][color]
+        cut = GROUPS[group][1]
+        rows = pl.ds(0, cut) if half == 0 else pl.ds(cut, block.shape[0] - cut)
+        return rows, pl.ds(start, size)
+
     def region(group, color, half, spot):
         wy, wz, wx = (spot[axis] for axis in ("y", "z", "x"))
         low, high = (slice(None), slice(None)) if wx is None else (lax.rem(wx, 2), wx // 2)
         wy = slice(None) if wy is None else wy
         wz = slice(None) if wz is None else wz
-        return weight.at[group, low, wy, wz, high, :, pl.ds((color * 2 + half) * unit, unit)]
+        return weight.at[(low, wy, wz, high) + part_of(group, color, half)]
 
     def spot_of(color, stage, coordinate):
         spot = dict(here)
@@ -163,7 +216,7 @@
         target = region(group, color, half, spot_of(color, stage, near(axis, offset)))
         source = target
         if stage == 0 and offset == 0:
-            source = block.at[:, pl.ds(group * group_width + (color * 2 + half) * unit, unit)]
+            source = block.at[part_of(group, color, half)]
         return remote(
             source, target, gather_send.at[group, color, stage, slot],
             gather_recv.at[group, color, stage, slot], along(axis, step),
@@ -200,52 +253,106 @@
 
     ring_start(0, 0)
     rows_copy.start()
-    for group in range(2):
-        weight[group, xl, y, z, xh] = block[:, group * group_width : (group + 1) * group_width]
+    weight[xl, y, z, xh] = block[...]
     ring_forward(0, 0)
     ring_start(0, 1)
     ring_start(1, 0)
+    lane = lax.broadcasted_iota(jnp.int32, (LANES, inner), 1)
+    first = lax.broadcasted_iota(jnp.int32, (LANES, inner), 0) * (inner // head_count)
+    ones = jnp.where(
+        jnp.logical_and(lane >= first, lane < first + inner // head_count), 1.0, 0.0
+    ).astype(BF16)
+    rows = lax.broadcasted_iota(jnp.int32, (CHUNK, LANES), 0)
+    columns = lax.broadcasted_iota(jnp.int32, (CHUNK, LANES), 1)
+    below = jnp.where(rows >= columns, 1.0, 0.0).astype(BF16)
+    for i in range(3):
+        spread_ref[i * LANES : (i + 1) * LANES, :] = ones
+        tri_ref[:, i * LANES : (i + 1) * LANES] = below
     ring_forward(0, 1)
     ring_forward(1, 0)
     ring_start(0, 2)
+    ring_start(1, 1)
+    skips[...] = dot(jnp.concatenate(split3(heads[...]), axis=1), spread_ref[...])
     ring_forward(0, 2)
-    ring_start(1, 1)
+    ring_forward(1, 1)
+    ring_start(1, 2)
+    ring_start(2, 0)
     own_rows.wait()
     rows_copy.wait_send()
     remote(
-        tokens_ref, rows_in.at[1 - core, pl.ds(HALO, slots)], token_send, token_recv, partner
+        shard, rows_in.at[1 - core, pl.ds(HALO, slots)], token_send, token_recv, partner
     ).wait_recv()
-    remote(live_ref, live.at[1 - core], live_send, live_recv, partner).wait_recv()
+    remote(live.at[core], live.at[1 - core], live_send, live_recv, partner).wait_recv()
 
     @pl.when(me > 0)
     def _():
         for side in range(2):
             remote(
-                edge_ref, rows_in.at[side, pl.ds(0, HALO)], edge_send.at[side], edge_recv.at[side],
+                edge, rows_in.at[side, pl.ds(0, HALO)], edge_send.at[side], edge_recv.at[side],
                 partner,
             ).wait_recv()
 
     ring_finish(0)
 
-    def project(group, first, last):
+    def matrix(start):
+        picked = pl.ds(pl.multiple_of(start, LANES), LANES)
+        pair = [weight[i, :, :, :, :, picked].reshape(model, LANES) for i in range(2)]
+        return jnp.concatenate(pair, axis=1)
+
+    def both_lanes(ref, row, starts):
+        return jnp.concatenate([ref[row : row + 1, pl.ds(start, LANES)] for start in starts], axis=1)
+
+    def project_mixed(group, seq, color):
+        result = dot(rows_in[seq], matrix(GROUPS[group][0][0][0] + color * LANES)).astype(BF16)
+        tiles = [group * 6 + color, group * 6 + color + 3]
+        if group == 0:
+            raw_all[seq, jnp.where(color == 1, 1, 0)] = result[HALO:, 0:LANES]
+        lanes = [
+            pl.multiple_of(
+                jnp.where(
+                    tile == 0, model + core * LANES, core * inner + jnp.maximum(tile - 2, 0) * LANES
+                ),
+                LANES,
+            )
+            for tile in tiles
+        ]
+        mixed = result.astype(F32)
+        conv = both_lanes(bias_ref, 0, lanes)
+        for k in range(4):
+            conv = conv + both_lanes(taps_ref, k, lanes) * mixed[HALO - 3 + k : HALO - 3 + k + slots]
+        act = (conv * jax.nn.sigmoid(conv)).astype(BF16)
+        for i, tile in enumerate(tiles):
+            act_all[seq, :, pl.ds(pl.multiple_of(tile * LANES, LANES), LANES)] = act[
+                :, i * LANES : (i + 1) * LANES
+            ]
+
+    def project_gate(first, last):
         @pl.loop(first, last)
         def _(i):
-            seq = lax.rem(i, 2)
-            tile = i // 2
-            columns = pl.ds(pl.multiple_of(lax.rem(tile, 3) * 2 * LANES, LANES), 2 * LANES)
-            matrix = weight[group, tile // 3, :, :, :, :, columns].reshape(model, 2 * LANES)
-            proj[seq, :, pl.ds(pl.multiple_of(tile * 2 * LANES, LANES), 2 * LANES)] = dot(
-                rows_in[seq], matrix
-            ).astype(BF16)
-
-    map_copy = remote(proj.at[:, :, pl.ds(0, LANES)], far_map, map_send, map_recv, partner)
-    project(0, 0, 4)
-    map_copy.start()
-    ring_forward(1, 1)
-    project(0, 4, 8)
-    ring_start(1, 2)
-    project(0, 8, 12)
-    map_copy.wait()
+            seq = i // 5
+            color = lax.rem(i, 5)
+            result = dot(rows_in[seq, HALO:, :], matrix(GROUPS[2][0][0][0] + color * LANES))
+            for half in range(2):
+                tile = pl.ds(pl.multiple_of((half * 5 + color) * LANES, LANES), LANES)
+                act_all[seq, :, tile] = result[:, half * LANES : (half + 1) * LANES].astype(BF16)
+
+    map_copy = remote(act_all.at[:, :, pl.ds(0, LANES)], far_map, map_send, map_recv, partner)
+
+    @pl.loop(0, 6)
+    def _(i):
+        project_mixed(0, lax.rem(i, 2), i // 2)
+
+        @pl.when(i == 2)
+        def _():
+            ring_forward(1, 2)
+            ring_forward(2, 0)
+            ring_start(2, 1)
+
+        @pl.when(i == 3)
+        def _():
+            map_copy.start()
+
+    ring_finish(1)
 
     def slice_of(ref, seq, k):
         row = pl.multiple_of(k // 2 * 8, 8)
@@ -277,43 +384,23 @@
             back_recv.at[seq * OWNERS + k], device(index),
         )
 
-    rows = lax.broadcasted_iota(jnp.int32, (CHUNK, LANES), 0)
-    columns = lax.broadcasted_iota(jnp.int32, (CHUNK, LANES), 1)
-
-    def wide_row(index):
-        return jnp.concatenate(
-            [params_ref[index : index + 1, pl.ds(core_lane, inner)], params_ref[index : index + 1, model:]],
-            axis=1,
-        )
-
     def scan_chunk(seq, chunk):
         row0 = pl.multiple_of(chunk * CHUNK, CHUNK)
-        window = pl.ds(row0, CHUNK + HALO)
-        near_map = proj[seq, window, 0:LANES].astype(F32)
-        other_map = far_map[seq, window, :].astype(F32)
-        mixed = jnp.concatenate(
-            [
-                proj[seq, window, 2 * LANES :].astype(F32),
-                jnp.where(core == 0, near_map, other_map),
-                jnp.where(core == 0, other_map, near_map),
-            ],
-            axis=1,
-        )
-        conv = wide_row(4)
-        for k in range(4):
-            conv = conv + wide_row(k) * mixed[HALO - 3 + k : HALO - 3 + k + CHUNK]
-        act = (conv * jax.nn.sigmoid(conv)).astype(BF16)
-        value = act[:, :inner]
-        in_map = act[:, inner : inner + LANES]
-        out_map = act[:, inner + LANES :]
-
-        raw = proj[seq, pl.ds(row0 + HALO, CHUNK), LANES : 2 * LANES].astype(F32)
-        raw = raw + heads_ref[core, 0:1, :]
+        window = pl.ds(row0, CHUNK)
+        near_map = act_all[seq, window, 0:LANES]
+        other_map = far_map[seq, window, :]
+        in_map = jnp.where(core == 0, near_map, other_map)
+        out_map = jnp.where(core == 0, other_map, near_map)
+        value = act_all[seq, window, 2 * LANES :]
+
+        raw = raw_all[seq, 1, window, :].astype(F32)
+        raw = jnp.where(core == 0, raw, pltpu.roll(raw, LANES - head_count, 1))
+        raw = raw + heads[0:1, :]
         tail = jnp.exp(-jnp.abs(raw))
         series = tail * (1.0 - tail * (0.5 - tail * (1.0 / 3.0 - 0.25 * tail)))
         step = jnp.maximum(raw, 0.0) + jnp.where(tail < 0.01, series, jnp.log(1.0 + tail))
         step = jnp.where((rows + row0).astype(F32) < live[seq, 0:1, :], step, 0.0)
-        log_decay = -(step * heads_ref[core, 1:2, :]) * LOG2E
+        log_decay = -(step * heads[1:2, :]) * LOG2E
         cum = dot(tri_ref[...], jnp.concatenate(split3(log_decay), axis=0))
         shifted = jnp.where(step > 0.0, cum - jnp.log(step) * LOG2E, 1e30).T
         causal = rows >= columns
@@ -325,7 +412,7 @@
         reach = dot(
             jnp.concatenate([out_map, out_map], axis=1), jnp.concatenate(split2(before), axis=0)
         )
-        base = growth * reach + params_ref[6:7, pl.ds(core_lane, inner)] * value.astype(F32)
+        base = growth * reach + skips[2:3, :] * value.astype(F32)
         left = columns < LANES // 2
         zero = jnp.zeros((CHUNK, LANES), BF16)
         for tile in range(inner // LANES):
@@ -359,31 +446,6 @@
         cum_all[seq, pl.ds(row0, CHUNK), :] = cum + total[seq]
         total[seq] = total[seq] + last
 
-    state[...] = jnp.zeros_like(state)
-    total[...] = jnp.zeros_like(total)
-    ring_forward(1, 2)
-
-    @pl.loop(0, 2)
-    def _(seq):
-        @pl.loop(0, slots // CHUNK)
-        def _(chunk):
-            scan_chunk(seq, chunk)
-
-        @pl.loop(0, OWNERS)
-        def _(i):
-            k = lax.rem(my_k + i, OWNERS)
-            mine = jnp.logical_and(i == 0, seq == my_seq)
-
-            @pl.when(jnp.logical_not(mine))
-            def _():
-                decay_copy(seq, k, me).start()
-                piece(seq, k, me).start()
-
-            @pl.when(mine)
-            def _():
-                arrived[me] = slice_of(state, seq, k)[...]
-                decays[me] = total[seq]
-
     def compose_all():
         @pl.loop(1, COUNT)
         def _(i):
@@ -409,11 +471,52 @@
 
         slice_of(incoming, my_seq, my_k)[...] = starts[me]
 
-    pl.when(my_seq == 0)(compose_all)
-    ring_finish(1)
-    project(1, 0, 4)
+    state[...] = jnp.zeros_like(state)
+    total[...] = jnp.zeros_like(total)
+
+    @pl.loop(0, 2)
+    def _(seq):
+        @pl.loop(0, 3)
+        def _(color):
+            project_mixed(1, seq, color)
+
+        @pl.when(seq == 0)
+        def _():
+            ring_forward(2, 1)
+            ring_start(2, 2)
+            map_copy.wait()
+
+        @pl.loop(0, slots // CHUNK)
+        def _(chunk):
+            scan_chunk(seq, chunk)
+
+            @pl.when(jnp.logical_and(jnp.logical_and(seq == 1, chunk == 3), my_seq == 0))
+            def _():
+                compose_all()
+
+        @pl.when(seq == 0)
+        def _():
+            ring_forward(2, 2)
+
+        @pl.loop(0, OWNERS)
+        def _(i):
+            k = lax.rem(my_k + i, OWNERS)
+            mine = jnp.logical_and(i == 0, seq == my_seq)
+
+            @pl.when(jnp.logical_not(mine))
+            def _():
+                decay_copy(seq, k, me).start()
+                piece(seq, k, me).start()
+
+            @pl.when(mine)
+            def _():
+                arrived[me] = slice_of(state, seq, k)[...]
+                decays[me] = total[seq]
+
+    ring_finish(2)
+    project_gate(0, 8)
     pl.when(my_seq == 1)(compose_all)
-    project(1, 4, 10)
+    project_gate(8, 10)
 
     def square_copy(seq):
         return remote(
@@ -439,7 +542,7 @@
             )
             out_map = map_all[seq, here_rows, :]
             reach = dot(jnp.concatenate([out_map, out_map], axis=1), start)
-            gate = proj[seq, pl.ds(row0 + HALO, CHUNK), 0:inner].astype(F32)
+            gate = act_all[seq, here_rows, 0:inner].astype(F32)
             gated = (y_all[seq, here_rows, :] + growth * reach) * (gate * jax.nn.sigmoid(gate))
             y_all[seq, here_rows, :] = gated
             square[seq, here_rows, :] = jnp.broadcast_to(
@@ -461,7 +564,7 @@
             result = (
                 y_all[seq, here_rows, :]
                 * lax.rsqrt(mean + 1e-05)
-                * params_ref[5:6, pl.ds(core_lane, inner)]
+                * gain_ref[0:1, pl.ds(core_lane, inner)]
             )
             kept = (rows[:, 0:1] + row0).astype(F32) < live[seq, 0:1, 0:1]
             return jnp.where(kept, result, 0.0).astype(BF16)
@@ -491,7 +594,7 @@
         for side in range(2):
             edge_copy(side).wait_send()
 
-    for group in range(2):
+    for group in range(3):
         for stage in range(3):
             for color in range(3):
                 for slot in range(6):
@@ -520,30 +623,43 @@
     ).wait_recv()
 
 
-def layer_call(live, edge, tokens, pieces, params, heads, spread, tri):
-    slots, model = tokens.shape
+def local(
+    tokens, bounds, in_weight, conv_weight, conv_bias, dt_bias, decay_rate, skip_gain, norm_gain
+):
+    slots, model = tokens.shape[1:]
     inner = model // 2
-    columns = pieces.shape[2]
+    rows = in_weight.shape[0]
     padded = slots + HALO
+    columns = 11 * LANES
     vmem = pl.BlockSpec(memory_space=pltpu.VMEM)
     dma = pltpu.SemaphoreType.DMA
-    return pl.pallas_call(
+    out = pl.pallas_call(
         layer_kernel,
         out_shape=jax.ShapeDtypeStruct((slots, model), BF16),
-        in_specs=[vmem, vmem, pl.BlockSpec(memory_space=pl.ANY)] + [vmem] * 5,
+        in_specs=[
+            pl.BlockSpec(memory_space=pltpu.SMEM), pl.BlockSpec(memory_space=pl.ANY),
+        ] + [vmem] * 7,
         out_specs=vmem,
         scratch_shapes=[
             pltpu.VMEM((2, padded, model), BF16),
-            pltpu.VMEM((2, 2, 4, 4, 2, model // 32, columns // 2), BF16),
-            pltpu.VMEM((2, padded, columns), BF16),
-            pltpu.VMEM((2, padded, LANES), BF16),
+            pltpu.VMEM((2, 4, 4, 2, 4 * rows, columns), BF16),
+            pltpu.VMEM((2, slots, 12 * LANES), BF16),
+            pltpu.VMEM((2, 2, slots, LANES), BF16),
+            pltpu.VMEM((3 * LANES, inner), BF16),
+            pltpu.VMEM((CHUNK, 3 * LANES), BF16),
+            pltpu.VMEM((8, LANES), F32),
+            pltpu.VMEM((8, inner), F32),
+            pltpu.VMEM((4, rows, columns), BF16),
+            pltpu.VMEM((slots // BLOCK, HALO, model), BF16),
+            pltpu.VMEM((HALO, model), BF16),
+            pltpu.VMEM((2, slots, LANES), BF16),
             pltpu.VMEM((2, slots, inner), F32),
             pltpu.VMEM((2, slots, LANES), BF16),
             pltpu.VMEM((2, slots, LANES), F32),
             pltpu.VMEM((2, LANES, inner), F32),
             pltpu.VMEM((2, 1, LANES), F32),
-            pltpu.VMEM(pieces.shape, BF16),
-            pltpu.VMEM((model // 32, columns), BF16),
+            pltpu.VMEM((4, rows, columns), BF16),
+            pltpu.VMEM((4 * rows, columns), BF16),
             pltpu.VMEM((COUNT, 8, inner // 2), F32),
             pltpu.VMEM((COUNT, 8, inner // 2), F32),
             pltpu.VMEM((COUNT, 1, LANES), F32),
@@ -553,11 +669,12 @@
             pltpu.VMEM((2, slots, LANES), F32),
             pltpu.VMEM((slots, inner), BF16),
             pltpu.VMEM((2, 8, LANES), F32),
+            dma((slots // BLOCK,)),
             dma((4,)), dma((4,)),
             dma, dma, dma,
             dma((2,)), dma((2,)),
             dma, dma,
-            dma((2, 3, 3, 6)), dma((2, 3, 3, 6)),
+            dma((3, 3, 3, 6)), dma((3, 3, 3, 6)),
             dma, dma,
             dma((COUNT,)), dma((COUNT,)), dma((COUNT,)), dma((COUNT,)),
             dma((COUNT,)), dma((COUNT,)),
@@ -568,57 +685,10 @@
             collective_id=0, has_side_effects=True, vmem_limit_bytes=67043328
         ),
         name="layer",
-    )(live, edge, tokens, pieces, params, heads, spread, tri)
-
-
-def local(
-    tokens, bounds, in_weight, conv_weight, conv_bias, dt_bias, decay_rate, skip_gain, norm_gain
-):
-    slots, model = tokens.shape[1:]
-    width = norm_gain.shape[0]
-    inner = width // 2
-    heads = decay_rate.shape[0] // 2
-    rows = in_weight.shape[0]
-
-    low, high = 4 * LANES, 6 * LANES
-    pieces = []
-    for side in range(2):
-        for core in range(2):
-            value = width + core * inner
-            gate = core * inner
-            if side == 0:
-                raw = 2 * width + 2 * LANES + core * heads
-                pieces += [
-                    in_weight[:, 2 * width + core * LANES : 2 * width + (core + 1) * LANES],
-                    jnp.pad(in_weight[:, raw : raw + heads], ((0, 0), (0, LANES - heads))),
-                    in_weight[:, value : value + low],
-                    in_weight[:, gate : gate + high],
-                ]
-            else:
-                pieces += [
-                    in_weight[:, value + low : value + inner],
-                    in_weight[:, gate + high : gate + inner],
-                    jnp.zeros((rows, 2 * high - inner), BF16),
-                ]
-    pieces = jnp.concatenate(pieces, axis=1).reshape(rows, 4, 2 * high).swapaxes(0, 1)
-
-    blocks = bounds[0, 0, 1] - bounds[0, 0, 0]
-    edge = lax.dynamic_slice_in_dim(tokens[0], blocks * BLOCK - HALO, HALO, 0)
-    live = jnp.full((8, LANES), (blocks * BLOCK).astype(F32))
-    stretch = lambda a: jnp.pad(a, (0, conv_bias.shape[0] - width))[None]
-    params = jnp.concatenate(
-        [
-            conv_weight, conv_bias[None], stretch(norm_gain),
-            stretch(jnp.repeat(skip_gain, width // (2 * heads))),
-            jnp.zeros((1, conv_bias.shape[0]), F32),
-        ]
+    )(
+        bounds, tokens, in_weight, conv_weight, conv_bias[None], dt_bias[None], decay_rate[None],
+        skip_gain[None], norm_gain[None],
     )
-    per_head = jnp.stack([dt_bias.reshape(2, heads), decay_rate.reshape(2, heads)], axis=1)
-    per_head = jnp.pad(per_head, ((0, 0), (0, 6), (0, LANES - heads)))
-    spread = (np.arange(inner)[None, :] // (inner // heads) == np.arange(LANES)[:, None])
-    spread = jnp.asarray(np.concatenate([spread] * 3, axis=0), BF16)
-    tri = jnp.asarray(np.concatenate([np.tril(np.ones((CHUNK, CHUNK)))] * 3, axis=1), BF16)
-    out = layer_call(live, edge, tokens[0], pieces, params, per_head, spread, tri)
     return out[None]
 
 

time: 186 us -> 169 us (0.909)
  local copies, waits for them, and re-layouts: 22.2 us -> 6.91 us
    unnamed x14 -> x1, local copies, waits for them, and re-layouts: 11.8 us -> 4.29 us
    slice x2 -> x0, local copies, waits for them, and re-layouts: 2.18 us -> none  [the longest x1 1.34 us: local(): blocks = bounds[0, 0, 1] - bounds[0, 0, 0]]
where the time goes in v3:
time: 169 us
  Pallas kernels  162 us (96%)
  local copies, waits for them, and re-layouts  6.91 us (4%)
    pallas_call x1, Pallas kernels, local(): pl.pallas_call(layer_kernel, out_shape=jax.ShapeDtypeStruct((slots, model...  162 us
    unnamed x1, local copies, waits for them, and re-layouts  4.29 us

profile of v3, /device:TPU:1, one launch (start us, length us, event | category | flops | bytes accessed | tf_op | source)
XLA Modules:
  0.0 168.6 jit_solution(2598729589201675331)
XLA Ops:
  0.0 1.3 broadcast_in_dim.22.gain_ref
  1.3 1.3 broadcast_in_dim.18.bias_ref
  2.6 161.7 %layer.1 = bf16[768,2560]{1,0:T(8,128)(2,1)} custom-call(s32[1,1,2]{2,1,0:T(1,128)} %bounds_ref.1, bf16[1,768,2560]{2,1,0:T(8,128)(2,1)} %tokens_ref.1, bf16[20,5416]{1,0:T(8,128)(2,1)} %shard_ref.1, f32[4,2816]{1,0:T(4,128)} %taps_ref.1, f32[1,2816]{1,0:T(1,128)} %broadcast_in_dim.18.bias_ref, f32[1,40]{1,0:T(1,128)} %bitcast.5, f32[1,40]{1,0:T(1,128)} %bitcast.6, ...), custom_call_target="tpu_custom_call" | custom-call | tf_op jit(solution)/shard_map/layer/pallas_call | solution.py:636
  164.3 4.3 %copy.11 = bf16[1,768,2560]{2,1,0:T(8,128)(2,1)} copy(bf16[1,768,2560]{2,1,0:T(8,128)(2,1)} %bitcast.4) | data formatting | bytes 7864320

commit v4 on v3

--- a/solution.py
+++ b/solution.py
@@ -18,10 +18,11 @@
 BF16 = jnp.bfloat16
 MESH = pl.DeviceIdType.MESH
 ORDERS = (("x", "y", "z"), ("y", "z", "x"), ("z", "x", "y"))
+CUT = 48
 GROUPS = (
-    (((0, 128), (128, 128), (256, 128)), 48),
-    (((384, 128), (512, 128), (640, 128)), 32),
-    (((768, 256), (1024, 256), (1280, 128)), 48),
+    ((0, 1), (1, 1), (2, 1)),
+    ((3, 1), (4, 1), (5, 1)),
+    ((6, 2), (8, 2), (10, 1)),
 )
 SLOTS = ((0, 0, 1), (0, 1, 1), (-1, 0, 1), (0, 1, -1), (0, 0, -1), (1, 1, -1))
 
@@ -47,9 +48,9 @@
 def layer_kernel(
     bounds_ref, tokens_ref, shard_ref, taps_ref, bias_ref, dt_ref, decay_ref, skip_ref, gain_ref,
     out_ref,
-    rows_in, weight, act_all, raw_all, spread_ref, tri_ref, heads, skips, pieces, ends, edge,
-    far_map, y_all, map_all, cum_all, state, total, parts, block, arrived,
-    starts, decays, factors, incoming, square, far_square, staged, live,
+    rows_in, top, bottom, act_all, raw_all, spread_ref, tri_ref, heads, skips, pieces, ends, edge,
+    far_map, y_all, map_all, cum_all, state, total, parts, arrived,
+    starts, decays, factors, incoming, square, far_square, staged, live, lift,
     end_sem, part_send, part_recv, token_sem, token_send, token_recv, edge_send, edge_recv, live_send,
     live_recv, gather_send, gather_recv, map_send, map_recv, piece_send, piece_recv, decay_send,
     decay_recv, back_send, back_recv, square_send, square_recv, out_send, out_recv,
@@ -180,7 +181,11 @@
 
     for step in (1, 2, 3):
         part_arrival(step).wait_recv()
-    block[...] = jnp.concatenate([parts[i].astype(F32) for i in range(4)], axis=0).astype(BF16)
+    block = jnp.concatenate([parts[i].astype(F32) for i in range(4)], axis=0).astype(BF16)
+    for tile in range(top.shape[0]):
+        lanes = slice(tile * LANES, (tile + 1) * LANES)
+        top[tile, y, z, xh, xl] = block[0:CUT, lanes]
+        bottom[tile, y, z, xh, xl] = block[CUT:, lanes]
 
     near = lambda axis, step: lax.rem(here[axis] + step + 4, 4)
 
@@ -190,18 +195,15 @@
             return {"xh": coordinate // 2, "xl": lax.rem(coordinate, 2)}
         return {axis: coordinate}
 
-    def part_of(group, color, half):
-        start, size = GROUPS[group][0][color]
-        cut = GROUPS[group][1]
-        rows = pl.ds(0, cut) if half == 0 else pl.ds(cut, block.shape[0] - cut)
-        return rows, pl.ds(start, size)
-
     def region(group, color, half, spot):
         wy, wz, wx = (spot[axis] for axis in ("y", "z", "x"))
-        low, high = (slice(None), slice(None)) if wx is None else (lax.rem(wx, 2), wx // 2)
+        high, low = (slice(None), slice(None)) if wx is None else (wx // 2, lax.rem(wx, 2))
         wy = slice(None) if wy is None else wy
         wz = slice(None) if wz is None else wz
-        return weight.at[(low, wy, wz, high) + part_of(group, color, half)]
+        first, tiles = GROUPS[group][color]
+        first = first if tiles == 1 else pl.ds(first, tiles)
+        ref = bottom if half == (group != 1) else top
+        return ref.at[first, wy, wz, high, low]
 
     def spot_of(color, stage, coordinate):
         spot = dict(here)
@@ -214,11 +216,8 @@
         offset, half, step = SLOTS[slot]
         axis = ORDERS[color][stage]
         target = region(group, color, half, spot_of(color, stage, near(axis, offset)))
-        source = target
-        if stage == 0 and offset == 0:
-            source = block.at[part_of(group, color, half)]
-        return remote(
-            source, target, gather_send.at[group, color, stage, slot],
+        return remote(
+            target, target, gather_send.at[group, color, stage, slot],
             gather_recv.at[group, color, stage, slot], along(axis, step),
         )
 
@@ -253,7 +252,6 @@
 
     ring_start(0, 0)
     rows_copy.start()
-    weight[xl, y, z, xh] = block[...]
     ring_forward(0, 0)
     ring_start(0, 1)
     ring_start(1, 0)
@@ -293,31 +291,39 @@
             ).wait_recv()
 
     ring_finish(0)
-
-    def matrix(start):
-        picked = pl.ds(pl.multiple_of(start, LANES), LANES)
-        pair = [weight[i, :, :, :, :, picked].reshape(model, LANES) for i in range(2)]
+    ring_forward(2, 0)
+    ring_start(2, 1)
+
+    def matrix(tile):
+        pair = [
+            jnp.concatenate(
+                [
+                    top[tile, :, :, :, i].reshape(-1, CUT, LANES),
+                    bottom[tile, :, :, :, i].reshape(-1, model // 32 - CUT, LANES),
+                ],
+                axis=1,
+            ).reshape(model, LANES)
+            for i in range(2)
+        ]
         return jnp.concatenate(pair, axis=1)
 
     def both_lanes(ref, row, starts):
         return jnp.concatenate([ref[row : row + 1, pl.ds(start, LANES)] for start in starts], axis=1)
 
     def project_mixed(group, seq, color):
-        result = dot(rows_in[seq], matrix(GROUPS[group][0][0][0] + color * LANES)).astype(BF16)
+        result = dot(rows_in[seq], matrix(GROUPS[group][0][0] + color)).astype(BF16)
         tiles = [group * 6 + color, group * 6 + color + 3]
         if group == 0:
             raw_all[seq, jnp.where(color == 1, 1, 0)] = result[HALO:, 0:LANES]
-        lanes = [
-            pl.multiple_of(
-                jnp.where(
-                    tile == 0, model + core * LANES, core * inner + jnp.maximum(tile - 2, 0) * LANES
-                ),
-                LANES,
+        spots = [
+            jnp.where(
+                tile == 0, model // LANES + core, core * (inner // LANES) + jnp.maximum(tile - 2, 0)
             )
             for tile in tiles
         ]
+        lanes = [pl.multiple_of(spot * LANES, LANES) for spot in spots]
         mixed = result.astype(F32)
-        conv = both_lanes(bias_ref, 0, lanes)
+        conv = jnp.concatenate([bias_ref[pl.ds(spot, 1), :] for spot in spots], axis=1)
         for k in range(4):
             conv = conv + both_lanes(taps_ref, k, lanes) * mixed[HALO - 3 + k : HALO - 3 + k + slots]
         act = (conv * jax.nn.sigmoid(conv)).astype(BF16)
@@ -331,7 +337,7 @@
         def _(i):
             seq = i // 5
             color = lax.rem(i, 5)
-            result = dot(rows_in[seq, HALO:, :], matrix(GROUPS[2][0][0][0] + color * LANES))
+            result = dot(rows_in[seq, HALO:, :], matrix(GROUPS[2][0][0] + color))
             for half in range(2):
                 tile = pl.ds(pl.multiple_of((half * 5 + color) * LANES, LANES), LANES)
                 act_all[seq, :, tile] = result[:, half * LANES : (half + 1) * LANES].astype(BF16)
@@ -342,15 +348,15 @@
     def _(i):
         project_mixed(0, lax.rem(i, 2), i // 2)
 
-        @pl.when(i == 2)
+        @pl.when(i == 1)
         def _():
             ring_forward(1, 2)
-            ring_forward(2, 0)
-            ring_start(2, 1)
-
-        @pl.when(i == 3)
+            ring_forward(2, 1)
+
+        @pl.when(i == 4)
         def _():
             map_copy.start()
+            ring_start(2, 2)
 
     ring_finish(1)
 
@@ -482,21 +488,15 @@
 
         @pl.when(seq == 0)
         def _():
-            ring_forward(2, 1)
-            ring_start(2, 2)
             map_copy.wait()
 
         @pl.loop(0, slots // CHUNK)
         def _(chunk):
             scan_chunk(seq, chunk)
 
-            @pl.when(jnp.logical_and(jnp.logical_and(seq == 1, chunk == 3), my_seq == 0))
+            @pl.when(jnp.logical_and(seq == 0, chunk == 1))
             def _():
-                compose_all()
-
-        @pl.when(seq == 0)
-        def _():
-            ring_forward(2, 2)
+                ring_forward(2, 2)
 
         @pl.loop(0, OWNERS)
         def _(i):
@@ -514,24 +514,16 @@
                 decays[me] = total[seq]
 
     ring_finish(2)
-    project_gate(0, 8)
-    pl.when(my_seq == 1)(compose_all)
-    project_gate(8, 10)
+    project_gate(0, 10)
+    compose_all()
 
     def square_copy(seq):
         return remote(
             square.at[seq], far_square.at[seq], square_send.at[seq], square_recv.at[seq], partner
         )
 
-    def gate_sequence(seq):
-        @pl.loop(0, OWNERS)
-        def _(k):
-            @pl.when(jnp.logical_not(jnp.logical_and(k == my_k, my_seq == seq)))
-            def _():
-                back(me, seq, k).wait_recv()
-
-        start = jnp.concatenate(split2(incoming[seq]), axis=0)
-
+    @pl.loop(0, 2)
+    def _(seq):
         @pl.loop(0, slots // CHUNK)
         def _(chunk):
             row0 = pl.multiple_of(chunk * CHUNK, CHUNK)
@@ -540,10 +532,27 @@
                 jnp.concatenate(split3(jnp.exp2(cum_all[seq, here_rows, :])), axis=1),
                 spread_ref[...],
             )
+            gate = act_all[seq, here_rows, 0:inner].astype(F32)
+            gate = gate * jax.nn.sigmoid(gate)
+            y_all[seq, here_rows, :] = y_all[seq, here_rows, :] * gate
+            lift[seq, here_rows, :] = growth * gate
+
+    def gate_sequence(seq):
+        @pl.loop(0, OWNERS)
+        def _(k):
+            @pl.when(jnp.logical_not(jnp.logical_and(k == my_k, my_seq == seq)))
+            def _():
+                back(me, seq, k).wait_recv()
+
+        start = jnp.concatenate(split2(incoming[seq]), axis=0)
+
+        @pl.loop(0, slots // CHUNK)
+        def _(chunk):
+            row0 = pl.multiple_of(chunk * CHUNK, CHUNK)
+            here_rows = pl.ds(row0, CHUNK)
             out_map = map_all[seq, here_rows, :]
             reach = dot(jnp.concatenate([out_map, out_map], axis=1), start)
-            gate = act_all[seq, here_rows, 0:inner].astype(F32)
-            gated = (y_all[seq, here_rows, :] + growth * reach) * (gate * jax.nn.sigmoid(gate))
+            gated = y_all[seq, here_rows, :] + lift[seq, here_rows, :] * reach
             y_all[seq, here_rows, :] = gated
             square[seq, here_rows, :] = jnp.broadcast_to(
                 jnp.sum(gated * gated, axis=1, keepdims=True), (CHUNK, LANES)
@@ -551,21 +560,24 @@
 
         square_copy(seq).start()
 
-    for seq in range(2):
-        gate_sequence(seq)
-
-    out_copy = remote(staged, out_ref.at[:, pl.ds(core_lane, inner)], out_send, out_recv, partner)
-    for seq in range(2):
+    def out_copy(piece):
+        part = pl.ds(piece * BLOCK, BLOCK)
+        return remote(
+            staged.at[part], out_ref.at[part, pl.ds(core_lane, inner)], out_send.at[piece],
+            out_recv.at[piece], partner,
+        )
+
+    gain = jnp.concatenate(
+        [gain_ref[pl.ds(core * (inner // LANES) + i, 1), :] for i in range(inner // LANES)], axis=1
+    )
+
+    def finish_sequence(seq):
         square_copy(seq).wait_recv()
 
         def normed(row0):
             here_rows = pl.ds(row0, CHUNK)
             mean = (square[seq, here_rows, 0:1] + far_square[seq, here_rows, 0:1]) / model
-            result = (
-                y_all[seq, here_rows, :]
-                * lax.rsqrt(mean + 1e-05)
-                * gain_ref[0:1, pl.ds(core_lane, inner)]
-            )
+            result = y_all[seq, here_rows, :] * lax.rsqrt(mean + 1e-05) * gain
             kept = (rows[:, 0:1] + row0).astype(F32) < live[seq, 0:1, 0:1]
             return jnp.where(kept, result, 0.0).astype(BF16)
 
@@ -578,12 +590,18 @@
 
         @pl.when(core != seq)
         def _():
-            @pl.loop(0, slots // CHUNK)
-            def _(chunk):
-                row0 = pl.multiple_of(chunk * CHUNK, CHUNK)
-                staged[pl.ds(row0, CHUNK), :] = normed(row0)
-
-            out_copy.start()
+            for piece in range(slots // BLOCK):
+                @pl.loop(0, BLOCK // CHUNK)
+                def _(chunk):
+                    row0 = pl.multiple_of(piece * BLOCK + chunk * CHUNK, CHUNK)
+                    staged[pl.ds(row0, CHUNK), :] = normed(row0)
+
+                out_copy(piece).start()
+
+    for seq in range(2):
+        gate_sequence(seq)
+    for seq in range(2):
+        finish_sequence(seq)
 
     for step in (1, 2, 3):
         part_copy(step).wait_send()
@@ -616,11 +634,14 @@
 
     for seq in range(2):
         square_copy(seq).wait_send()
-    out_copy.wait_send()
     far_lane = pl.multiple_of((1 - core) * inner, LANES)
-    remote(
-        staged, out_ref.at[:, pl.ds(far_lane, inner)], out_send, out_recv, partner
-    ).wait_recv()
+    for piece in range(slots // BLOCK):
+        out_copy(piece).wait_send()
+        part = pl.ds(piece * BLOCK, BLOCK)
+        remote(
+            staged.at[part], out_ref.at[part, pl.ds(far_lane, inner)], out_send.at[piece],
+            out_recv.at[piece], partner,
+        ).wait_recv()
 
 
 def local(
@@ -642,7 +663,8 @@
         out_specs=vmem,
         scratch_shapes=[
             pltpu.VMEM((2, padded, model), BF16),
-            pltpu.VMEM((2, 4, 4, 2, 4 * rows, columns), BF16),
+            pltpu.VMEM((columns // LANES, 4, 4, 2, 2, CUT, LANES), BF16),
+            pltpu.VMEM((columns // LANES, 4, 4, 2, 2, 4 * rows - CUT, LANES), BF16),
             pltpu.VMEM((2, slots, 12 * LANES), BF16),
             pltpu.VMEM((2, 2, slots, LANES), BF16),
             pltpu.VMEM((3 * LANES, inner), BF16),
@@ -659,7 +681,6 @@
             pltpu.VMEM((2, LANES, inner), F32),
             pltpu.VMEM((2, 1, LANES), F32),
             pltpu.VMEM((4, rows, columns), BF16),
-            pltpu.VMEM((4 * rows, columns), BF16),
             pltpu.VMEM((COUNT, 8, inner // 2), F32),
             pltpu.VMEM((COUNT, 8, inner // 2), F32),
             pltpu.VMEM((COUNT, 1, LANES), F32),
@@ -669,6 +690,7 @@
             pltpu.VMEM((2, slots, LANES), F32),
             pltpu.VMEM((slots, inner), BF16),
             pltpu.VMEM((2, 8, LANES), F32),
+            pltpu.VMEM((2, slots, inner), F32),
             dma((slots // BLOCK,)),
             dma((4,)), dma((4,)),
             dma, dma, dma,
@@ -679,15 +701,15 @@
             dma((COUNT,)), dma((COUNT,)), dma((COUNT,)), dma((COUNT,)),
             dma((COUNT,)), dma((COUNT,)),
             dma((2,)), dma((2,)),
-            dma, dma,
+            dma((slots // BLOCK,)), dma((slots // BLOCK,)),
         ],
         compiler_params=pltpu.CompilerParams(
             collective_id=0, has_side_effects=True, vmem_limit_bytes=67043328
         ),
         name="layer",
     )(
-        bounds, tokens, in_weight, conv_weight, conv_bias[None], dt_bias[None], decay_rate[None],
-        skip_gain[None], norm_gain[None],
+        bounds, tokens, in_weight, conv_weight, conv_bias.reshape(-1, LANES), dt_bias[None], decay_rate[None],
+        skip_gain[None], norm_gain.reshape(-1, LANES),
     )
     return out[None]
 

time: 169 us -> 155 us (0.917)
  Pallas kernels: 162 us -> 151 us
  local copies, waits for them, and re-layouts: 6.91 us -> 4.29 us
    pallas_call x1, Pallas kernels: 162 us -> 151 us  [local(): pl.pallas_call(layer_kernel, out_shape=jax.ShapeDtypeStruct((slots, model...]
    broadcast_in_dim x2 -> x0, local copies, waits for them, and re-layouts: 2.62 us -> none  [the longest x1 1.31 us: local(): conv_bias[None]]
where the time goes in v4:
time: 155 us
  Pallas kernels  151 us (97%)
  local copies, waits for them, and re-layouts  4.29 us (3%)
    pallas_call x1, Pallas kernels, local(): pl.pallas_call(layer_kernel, out_shape=jax.ShapeDtypeStruct((slots, model...  151 us
    unnamed x1, local copies, waits for them, and re-layouts  4.29 us

profile of v4, /device:TPU:1, one launch (start us, length us, event | category | flops | bytes accessed | tf_op | source)
XLA Modules:
  0.0 154.9 jit_solution(787112297387625995)
XLA Ops:
  0.0 150.6 %layer.1 = bf16[768,2560]{1,0:T(8,128)(2,1)} custom-call(s32[1,1,2]{2,1,0:T(1,128)} %bounds_ref.1, bf16[1,768,2560]{2,1,0:T(8,128)(2,1)} %tokens_ref.1, bf16[20,5416]{1,0:T(8,128)(2,1)} %shard_ref.1, f32[4,2816]{1,0:T(4,128)} %taps_ref.1, f32[22,128]{1,0:T(8,128)} %bitcast.7, f32[1,40]{1,0:T(1,128)} %bitcast.9, f32[1,40]{1,0:T(1,128)} %bitcast.10, ...), custom_call_target="tpu_custom_call" | custom-call | tf_op jit(solution)/shard_map/layer/pallas_call | solution.py:657
  150.6 4.3 %copy.11 = bf16[1,768,2560]{2,1,0:T(8,128)(2,1)} copy(bf16[1,768,2560]{2,1,0:T(8,128)(2,1)} %bitcast.6) | data formatting | bytes 7864320
